TPU v7x, 8 devices: a whole 2x2x1 slice. The times are simulated.
8 devices in a mesh: data: 1 (over z), tp: 8 (over y, x, core).
Axes of the slice: x: 2, y: 2, z: 1, core: 2. Of those that a mesh axis runs over, the one named last changes fastest.
Arguments:
- x_in: bfloat16 [8192, 2048], P('data')
- w_gate: bfloat16 [2048, 8192], P(None, 'tp')
- w_up: bfloat16 [2048, 8192], P(None, 'tp')
- w_down: bfloat16 [8192, 2048], P('tp')
- residual: bfloat16 [8192, 2048], P(('data', 'tp'))
- norm_gain: float32 [2048], replicated
Outputs:
- output 1: bfloat16 [8192, 2048], P(('data', 'tp'))
- output 2: bfloat16 [8192, 2048], P(('data', 'tp'))
All inputs are finite; a program needn't handle non-finite values.
Results may differ from a plain program's by a relative error of at most 0.00647001.
Values are sent between devices in bfloat16 or wider.
A program may use at most 1 GiB of HBM per device.

v0:
```python
import jax
import jax.numpy as jnp
from jax import lax
from jax.sharding import PartitionSpec as P

EPS = 1e-5


def add_and_norm(y_sum, residual, norm_gain):
    hidden_sum = residual.astype(jnp.float32) + y_sum
    mean_sq = jnp.mean(hidden_sum * hidden_sum, axis=-1, keepdims=True)
    normed = hidden_sum * lax.rsqrt(mean_sq + EPS) * norm_gain
    return hidden_sum.astype(jnp.bfloat16), normed.astype(jnp.bfloat16)


def solution(mesh):
    tp_size = mesh.shape["tp"]

    def local_block(x_in, w_gate, w_up, w_down, residual, norm_gain):
        gate_val = jnp.dot(x_in, w_gate, preferred_element_type=jnp.float32)
        up_val = jnp.dot(x_in, w_up, preferred_element_type=jnp.float32)
        hidden = (jax.nn.silu(gate_val) * up_val).astype(jnp.bfloat16)
        part_prod = jnp.dot(hidden, w_down, preferred_element_type=jnp.float32).astype(jnp.bfloat16)
        received = lax.all_to_all(part_prod, "tp", 0, 0, tiled=True)
        rows = residual.shape[0]
        y_sum = jnp.sum(received.reshape(tp_size, rows, received.shape[1]), axis=0, dtype=jnp.float32)
        return add_and_norm(y_sum, residual, norm_gain)

    row_spec = P(("data", "tp"), None)
    return jax.shard_map(local_block, mesh=mesh, in_specs=(P("data", None), P(None, "tp"), P(None, "tp"), P("tp", None), row_spec, P(None)), out_specs=(row_spec, row_spec), check_vma=False)
```

profile of v0, /device:TPU:1, one launch (start us, length us, event | category | flops | bytes accessed | tf_op | source)
XLA Modules:
  0.0 537.9 jit_solution(2780584424860535846)
XLA Ops:
  0.6 42.3 %fusion.1 = f32[8192,1024]{1,0:T(8,128)} fusion(bf16[8192,2048]{1,0:T(8,128)(2,1)} %param.6, bf16[2048,1024]{1,0:T(8,128)(2,1)} %param.7), kind=kOutput, calls=%fused_computation.8 | convolution fusion | flops 34359738368 | bytes 71303168 | tf_op jit(solution)/shard_map/dot_general | solution.py:20
  42.9 48.8 %fusion.25 = bf16[8192,1024]{1,0:T(8,128)(2,1)} fusion(bf16[2048,1024]{1,0:T(8,128)(2,1)} %param.8, bf16[8192,2048]{1,0:T(8,128)(2,1)} %param.6, f32[8192,1024]{1,0:T(8,128)} %fusion.1), kind=kOutput, calls=%bitcast_fusion.1.clone.1 | convolution fusion | flops 34410070016 | bytes 88080384 | tf_op jit(solution)/shard_map/dot_general | solution.py:21
  91.7 45.1 %convolution_convert_fusion = bf16[8192,2048]{1,0:T(8,128)(2,1)} fusion(bf16[1024,2048]{1,0:T(8,128)(2,1)} %param.9, bf16[8192,1024]{1,0:T(8,128)(2,1)} %fusion.25), kind=kOutput, calls=%fused_computation.2 | convolution fusion | flops 34376515584 | bytes 54525952 | tf_op jit(solution)/shard_map/dot_general | solution.py:23
  136.8 372.9 %all_to_all.9 = bf16[8,1024,2048]{2,1,0:T(8,128)(2,1)} all-to-all(bf16[8,1024,2048]{2,1,0:T(8,128)(2,1)} %bitcast.26), channel_id=1, replica_groups=mesh['data'=1,'tp'=8] {'tp'}, dimensions={0} | all-to-all | bytes 67108864 | tf_op jit(solution)/shard_map/all_to_all | solution.py:24
  509.7 15.0 %convert_reduce_fusion = f32[1024,2048]{1,0:T(8,128)} fusion(bf16[8,1024,2048]{2,1,0:T(8,128)(2,1)} %all_to_all.9), kind=kLoop, calls=%fused_computation | loop fusion | flops 31457280 | bytes 41943040 | tf_op jit(solution)/shard_map/reduce_sum | solution.py:26
  524.7 0.0 copy-start
  524.7 0.0 copy-start.1
  524.7 0.0 copy-start.2
  524.7 5.9 %multiply_reduce_fusion = f32[1024]{0:T(1024)S(1)} fusion(f32[1024,2048]{1,0:T(8,128)} %convert_reduce_fusion, bf16[1024,2048]{1,0:T(8,128)(2,1)} %param.10), kind=kLoop, calls=%fused_computation.4 | loop fusion | flops 8387584 | bytes 12587008 | tf_op jit(solution)/shard_map/reduce_sum | solution.py:11
  530.6 1.1 copy-done
  531.7 1.2 copy-done.1
  532.9 0.0 copy-done.2
  532.9 5.0 multiply_convert_fusion.1
  (1 shorter events, 0.0 us)
Async XLA Ops:
  524.7 7.0 %copy-start = (f32[1024,2048]{1,0:T(8,128)S(1)}, f32[1024,2048]{1,0:T(8,128)}, u32[]{:S(2)}) copy-start(f32[1024,2048]{1,0:T(8,128)} %convert_reduce_fusion) | copy-start | bytes 25165828
  524.7 8.2 %copy-start.1 = (bf16[1024,2048]{1,0:T(8,128)(2,1)S(1)}, bf16[1024,2048]{1,0:T(8,128)(2,1)}, u32[]{:S(2)}) copy-start(bf16[1024,2048]{1,0:T(8,128)(2,1)} %param.10) | copy-start | bytes 12582916
  524.7 8.2 %copy-start.2 = (f32[2048]{0:T(1024)S(1)}, f32[2048]{0:T(1024)}, u32[]{:S(2)}) copy-start(f32[2048]{0:T(1024)} %param.11) | copy-start | bytes 24580
where the time goes:
time: 540 us; the launch traced here: 538 us
  blocking collectives  373 us (69%)
  matrix products  136 us (25%)
  other arithmetic  25.9 us (5%)
    all_to_all x1, blocking collectives, local_block(): received = lax.all_to_all(part_prod, 'tp', 0, 0, tiled=True)  373 us
    dot_general x1, matrix products, local_block(): up_val = jnp.dot(x_in, w_up, preferred_element_type=jnp.float32)  48.8 us
    dot_general x1, matrix products, local_block(): jnp.dot(hidden, w_down, preferred_element_type=jnp.float32)  45.1 us
    dot_general x1, matrix products, local_block(): gate_val = jnp.dot(x_in, w_gate, preferred_element_type=jnp.float32)  42.3 us
    reduce_sum x1, other arithmetic, local_block(): jnp.sum(received.reshape(tp_size, rows, received.shape[1]), axis=0, dtype...  15 us

commit v1 on v0

v1 whole, which is shorter than its diff:
```python
import functools

import jax
import jax.numpy as jnp
from jax import lax
from jax.experimental import pallas as pl
from jax.experimental.pallas import tpu as pltpu
from jax.sharding import PartitionSpec as P

EPS = 1e-5
ROWS = 256
HALF = 128
BLOCK = 1024
STEPS = BLOCK // ROWS
D = 2048
F = 1024
RELAY_SLOTS = 5
SUM_SLOTS = 3
FIRST = 2 * STEPS
SECOND = 4 * STEPS
TILES = 8 * STEPS


def kernel(x_hbm, wg_hbm, wu_hbm, wd_hbm, res_hbm, gain_ref, h_hbm, n_hbm, sum_in, x_buf, wg, wu, wd, hid, tiles, relay_in, sib_in, sum_out, sum_ld, res_ld, h_out, n_out,
           x_sem, w_sem, relay_ssem, relay_rsem, sib_ssem, sib_rsem, sum_ssem, sum_rsem, ld_sem, res_sem, out_sem):
    me = lax.axis_index("tp")
    c, cx, cy = me % 2, (me // 2) % 2, me // 4
    sib = cy * 4 + cx * 2 + (1 - c)
    xn = cy * 4 + (1 - cx) * 2
    yn = (1 - cy) * 4 + cx * 2

    barrier = pltpu.get_barrier_semaphore()
    for dev in (sib, xn, xn + 1, yn, yn + 1):
        pl.semaphore_signal(barrier, inc=1, device_id={"tp": dev}, device_id_type=pl.DeviceIdType.MESH)

    def row_of(i):
        first = 1 - (i + TILES - FIRST) // TILES
        last = (i + FIRST) // TILES
        mid = 1 - first - last
        p = i - FIRST
        q = p % 4
        direction = q % 2
        r = i - FIRST - SECOND
        ty = first * (1 - cy) + mid * (cy + direction * (1 - 2 * cy)) + last * cy
        tx = first * (1 - cx) + mid * (cx + (1 - direction) * (1 - 2 * cx)) + last * cx
        tc = first * (i % 2) + mid * ((1 - c) + (q // 2) * (2 * c - 1)) + last * ((1 - c) + ((r + TILES) // STEPS - TILES // STEPS) * (2 * c - 1))
        k = first * (i // 2) + mid * (p // 4) + last * (i % STEPS)
        return pl.multiple_of((ty * 4 + tx * 2 + tc) * BLOCK + k * ROWS, ROWS)

    def x_copy(i):
        return pltpu.make_async_copy(x_hbm.at[pl.ds(row_of(i), ROWS)], x_buf.at[i % 2], x_sem.at[i % 2])

    def w_copies():
        return [pltpu.make_async_copy(src, dst, w_sem.at[j]) for j, (src, dst) in enumerate(((wg_hbm, wg), (wu_hbm, wu), (wd_hbm, wd)))]

    x_copy(0).start()
    for copy in w_copies():
        copy.start()

    def relay_copy(i):
        via = (1 - c) * xn + c * yn + i % 2
        return pltpu.make_async_remote_copy(
            src_ref=tiles.at[i % RELAY_SLOTS], dst_ref=relay_in.at[1 - c, i // 2], send_sem=relay_ssem.at[i % RELAY_SLOTS],
            recv_sem=relay_rsem.at[1 - c, i // 2], device_id={"tp": via}, device_id_type=pl.DeviceIdType.MESH)

    def relay_arrival(group, k):
        return pltpu.make_async_remote_copy(
            src_ref=relay_in.at[group, k], dst_ref=relay_in.at[group, k], send_sem=relay_ssem.at[0],
            recv_sem=relay_rsem.at[group, k], device_id={"tp": sib}, device_id_type=pl.DeviceIdType.MESH)

    def sib_copy(slot, group, k):
        return pltpu.make_async_remote_copy(
            src_ref=tiles.at[RELAY_SLOTS + slot], dst_ref=sib_in.at[group, k], send_sem=sib_ssem.at[slot],
            recv_sem=sib_rsem.at[group, k], device_id={"tp": sib}, device_id_type=pl.DeviceIdType.MESH)

    def sum_copy(direction, k, half):
        slot = k % SUM_SLOTS
        to = (1 - direction) * xn + direction * yn + c
        return pltpu.make_async_remote_copy(
            src_ref=sum_out.at[direction, slot, pl.ds(half * HALF, HALF)], dst_ref=sum_in.at[direction, k, half],
            send_sem=sum_ssem.at[direction, slot, half], recv_sem=sum_rsem.at[direction, k, half],
            device_id={"tp": to}, device_id_type=pl.DeviceIdType.MESH)

    def ffn(x_ref, out_ref):
        for n in range(F // 256):
            cols = slice(n * 256, (n + 1) * 256)
            gate = jnp.dot(x_ref[...], wg[:, cols], preferred_element_type=jnp.float32)
            up = jnp.dot(x_ref[...], wu[:, cols], preferred_element_type=jnp.float32)
            hid[:, cols] = (gate * jax.nn.sigmoid(gate) * up).astype(jnp.bfloat16)
        for n in range(D // 512):
            cols = slice(n * 512, (n + 1) * 512)
            out_ref[:, cols] = jnp.dot(hid[...], wd[:, cols], preferred_element_type=jnp.float32).astype(jnp.bfloat16)

    for copy in w_copies():
        copy.wait()
    pl.semaphore_wait(barrier, 5)

    @pl.loop(0, TILES)
    def _(i):
        first = 1 - (i + TILES - FIRST) // TILES
        last = (i + FIRST) // TILES
        mid = 1 - first - last
        p = i - FIRST
        q = p % 4
        direction = q % 2
        k_mid = p // 4
        k_last = i % STEPS
        is_relay = i < FIRST
        is_sib = jnp.logical_and(i >= FIRST, jnp.logical_and(i < FIRST + SECOND, q < 2))
        is_sum = jnp.logical_and(i >= FIRST, jnp.logical_and(i < FIRST + SECOND, q >= 2))
        is_own_sib = jnp.logical_and(i >= FIRST + SECOND, i < FIRST + SECOND + STEPS)
        is_final = i >= FIRST + SECOND + STEPS
        sending = mid * (q // 2) + last * ((i - FIRST - SECOND + TILES) // STEPS - TILES // STEPS)
        slot = first * (i % RELAY_SLOTS) + (1 - first) * (RELAY_SLOTS + sending * 2 + (1 - sending) * (i % 2))

        @pl.when(i + 1 < TILES)
        def _():
            x_copy(i + 1).start()

        x_copy(i).wait()

        @pl.when(jnp.logical_and(is_relay, i >= RELAY_SLOTS))
        def _():
            relay_copy(i - RELAY_SLOTS).wait_send()

        @pl.when(jnp.logical_and(jnp.logical_or(is_sib, is_own_sib), i >= FIRST + 4))
        def _():
            sib_copy(i % 2, 0, 0).wait_send()

        @pl.when(is_final)
        def _():
            pltpu.make_async_copy(res_hbm.at[pl.ds(pl.multiple_of(k_last * ROWS, ROWS), ROWS)], res_ld, res_sem).start()

        ffn(x_buf.at[i % 2], tiles.at[slot])

        @pl.when(is_relay)
        def _():
            relay_copy(i).start()

        @pl.when(is_sib)
        def _():
            sib_copy(i % 2, direction, k_mid).start()

        @pl.when(is_own_sib)
        def _():
            sib_copy(i % 2, 2, k_last).start()

        @pl.when(is_sum)
        def _():
            sib_copy(0, direction, k_mid).wait_recv()
            relay_arrival(direction, k_mid).wait_recv()

            @pl.when(k_mid >= SUM_SLOTS)
            def _():
                for half in range(2):
                    sum_copy(direction, k_mid - SUM_SLOTS, half).wait_send()

            for half in range(2):
                @pl.loop(0, HALF // 16)
                def _(b):
                    rows = pl.ds(pl.multiple_of(half * HALF + b * 16, 16), 16)
                    total = tiles[RELAY_SLOTS + 2, rows].astype(jnp.float32) + sib_in[direction, k_mid, rows].astype(jnp.float32)
                    sum_out[direction, k_mid % SUM_SLOTS, rows] = total + relay_in[direction, k_mid, rows].astype(jnp.float32)

                sum_copy(direction, k_mid, half).start()

        @pl.when(is_final)
        def _():
            sib_copy(0, 2, k_last).wait_recv()
            pltpu.make_async_copy(res_hbm.at[pl.ds(0, ROWS)], res_ld, res_sem).wait()
            for half in range(2):
                for d in range(2):
                    sum_copy(d, k_last, half).wait_recv()
                loads = [pltpu.make_async_copy(sum_in.at[d, k_last, half], sum_ld.at[d], ld_sem.at[d]) for d in range(2)]
                for load in loads:
                    load.start()

                def stores(k):
                    rows = pl.ds(pl.multiple_of(k * ROWS + half * HALF, HALF), HALF)
                    return [pltpu.make_async_copy(h_out.at[half], h_hbm.at[rows], out_sem.at[half, 0]),
                            pltpu.make_async_copy(n_out.at[half], n_hbm.at[rows], out_sem.at[half, 1])]

                @pl.when(k_last > 0)
                def _():
                    for store in stores(k_last - 1):
                        store.wait()

                for load in loads:
                    load.wait()

                @pl.loop(0, HALF // 16)
                def _(b):
                    here = pl.ds(pl.multiple_of(b * 16, 16), 16)
                    rows = pl.ds(pl.multiple_of(half * HALF + b * 16, 16), 16)
                    y_sum = tiles[RELAY_SLOTS + 2, rows].astype(jnp.float32) + sib_in[2, k_last, rows].astype(jnp.float32)
                    y_sum = y_sum + (sum_ld[0, here] + sum_ld[1, here])
                    h = res_ld[rows].astype(jnp.float32) + y_sum
                    mean_sq = jnp.mean(h * h, axis=-1, keepdims=True)
                    h_out[half, here] = h.astype(jnp.bfloat16)
                    n_out[half, here] = (h * lax.rsqrt(mean_sq + EPS) * gain_ref[...]).astype(jnp.bfloat16)

                for store in stores(k_last):
                    store.start()

    for s in range(RELAY_SLOTS):
        relay_copy(FIRST - RELAY_SLOTS + s).wait_send()
    for s in range(2):
        sib_copy(s, 0, 0).wait_send()
    for d in range(2):
        for k in range(STEPS - SUM_SLOTS, STEPS):
            for half in range(2):
                sum_copy(d, k, half).wait_send()
    for half in range(2):
        rows = pl.ds((STEPS - 1) * ROWS + half * HALF, HALF)
        pltpu.make_async_copy(h_out.at[half], h_hbm.at[rows], out_sem.at[half, 0]).wait()
        pltpu.make_async_copy(n_out.at[half], n_hbm.at[rows], out_sem.at[half, 1]).wait()


def solution(mesh):
    def local_block(x_in, w_gate, w_up, w_down, residual, norm_gain):
        hbm = pl.BlockSpec(memory_space=pltpu.HBM)
        h, n, _ = pl.pallas_call(
            kernel,
            out_shape=(
                jax.ShapeDtypeStruct((BLOCK, D), jnp.bfloat16),
                jax.ShapeDtypeStruct((BLOCK, D), jnp.bfloat16),
                jax.ShapeDtypeStruct((2, STEPS, 2, HALF, D), jnp.float32),
            ),
            in_specs=[hbm] * 5 + [pl.BlockSpec(memory_space=pltpu.VMEM)],
            out_specs=(hbm, hbm, hbm),
            scratch_shapes=[
                pltpu.VMEM((2, ROWS, D), jnp.bfloat16),
                pltpu.VMEM((D, F), jnp.bfloat16),
                pltpu.VMEM((D, F), jnp.bfloat16),
                pltpu.VMEM((F, D), jnp.bfloat16),
                pltpu.VMEM((ROWS, F), jnp.bfloat16),
                pltpu.VMEM((RELAY_SLOTS + 3, ROWS, D), jnp.bfloat16),
                pltpu.VMEM((2, STEPS, ROWS, D), jnp.bfloat16),
                pltpu.VMEM((3, STEPS, ROWS, D), jnp.bfloat16),
                pltpu.VMEM((2, SUM_SLOTS, ROWS, D), jnp.float32),
                pltpu.VMEM((2, HALF, D), jnp.float32),
                pltpu.VMEM((ROWS, D), jnp.bfloat16),
                pltpu.VMEM((2, HALF, D), jnp.bfloat16),
                pltpu.VMEM((2, HALF, D), jnp.bfloat16),
                pltpu.SemaphoreType.DMA((2,)),
                pltpu.SemaphoreType.DMA((3,)),
                pltpu.SemaphoreType.DMA((RELAY_SLOTS,)),
                pltpu.SemaphoreType.DMA((2, STEPS)),
                pltpu.SemaphoreType.DMA((2,)),
                pltpu.SemaphoreType.DMA((3, STEPS)),
                pltpu.SemaphoreType.DMA((2, SUM_SLOTS, 2)),
                pltpu.SemaphoreType.DMA((2, STEPS, 2)),
                pltpu.SemaphoreType.DMA((2,)),
                pltpu.SemaphoreType.DMA,
                pltpu.SemaphoreType.DMA((2, 2)),
            ],
            compiler_params=pltpu.CompilerParams(collective_id=0, has_side_effects=True, vmem_limit_bytes=67000000),
            name="mlp_reduce",
        )(x_in, w_gate, w_up, w_down, residual, norm_gain.reshape(1, D))
        return h, n

    row_spec = P(("data", "tp"), None)
    return jax.shard_map(local_block, mesh=mesh, in_specs=(P("data", None), P(None, "tp"), P(None, "tp"), P("tp", None), row_spec, P(None)), out_specs=(row_spec, row_spec), check_vma=False)
```

time: 540 us -> 296 us (0.55)
  blocking collectives: 373 us -> 0 us
  Pallas kernels: 0 us -> 286 us
  matrix products: 136 us -> 0 us
  other arithmetic: 25.9 us -> 0 us
    all_to_all x1 -> x0, blocking collectives: 373 us -> none  [local_block(): received = lax.all_to_all(part_prod, 'tp', 0, 0, tiled=True)]
    pallas_call x0 -> x1, Pallas kernels: none -> 286 us  [local_block(): pl.pallas_call(kernel, out_shape=(jax.ShapeDtypeStruct((BLOCK, D), jnp.bf...]
    dot_general x3 -> x0, matrix products: 136 us -> none  [the longest x1 48.8 us: local_block(): up_val = jnp.dot(x_in, w_up, preferred_element_type=jnp.float32)]
    reduce_sum x2 -> x0, other arithmetic: 20.9 us -> none  [the longest x1 15 us: local_block(): jnp.sum(received.reshape(tp_size, rows, received.shape[1]), axis=0, dtype...]
where the time goes in v1:
time: 296 us; the launch traced here: 294 us
  Pallas kernels  286 us (97%)
  local copies, waits for them, and re-layouts  6.96 us (2%)
    pallas_call x1, Pallas kernels, local_block(): pl.pallas_call(kernel, out_shape=(jax.ShapeDtypeStruct((BLOCK, D), jnp.bf...  286 us
    unnamed x4, local copies, waits for them, and re-layouts  6.96 us

profile of v1, /device:TPU:1, one launch (start us, length us, event | category | flops | bytes accessed | tf_op | source)
XLA Modules:
  0.0 293.9 jit_solution(11929814447977498164)
XLA Ops:
  0.6 286.3 %mlp_reduce.1 = (bf16[1024,2048]{1,0:T(8,128)(2,1)}, bf16[1024,2048]{1,0:T(8,128)(2,1)}, f32[2,4,2,128,2048]{4,3,2,1,0:T(8,128)}) custom-call(bf16[8192,2048]{1,0:T(8,128)(2,1)} %x_hbm.1, bf16[2048,1024]{1,0:T(8,128)(2,1)} %wg_hbm.1, bf16[2048,1024]{1,0:T(8,128)(2,1)} %wu_hbm.1, bf16[1024,2048]{1,0:T(8,128)(2,1)} %wd_hbm.1, bf16[1024,2048]{1,0:T(8,128)(2,1)} %res_hbm.1, ...), custom_call_target="tpu_custom_call" | custom-call | tf_op jit(solution)/shard_map/mlp_reduce/pallas_call | solution.py:222
  286.9 0.0 copy-start
  286.9 4.9 %copy.10 = bf16[1024,2048]{1,0:T(8,128)(2,1)} copy(bf16[1024,2048]{1,0:T(8,128)(2,1)} %get-tuple-element.8) | data formatting | bytes 8388608
  291.9 0.0 copy-done
  291.9 2.0 copy.11
Async XLA Ops:
  286.9 5.0 %copy-start = (bf16[1024,2048]{1,0:T(8,128)(2,1)S(1)}, bf16[1024,2048]{1,0:T(8,128)(2,1)}, u32[]{:S(2)}) copy-start(bf16[1024,2048]{1,0:T(8,128)(2,1)} %get-tuple-element.9) | copy-start | bytes 12582916

commit v2 on v1

--- a/solution.py
+++ b/solution.py
@@ -9,20 +9,22 @@
 
 EPS = 1e-5
 ROWS = 256
+CHUNKS = 4
+COLS = (256, 256, 512)
 HALF = 128
 BLOCK = 1024
 STEPS = BLOCK // ROWS
 D = 2048
 F = 1024
-RELAY_SLOTS = 5
-SUM_SLOTS = 3
+RELAY_SLOTS = 3
+SUM_SLOTS = 2
 FIRST = 2 * STEPS
 SECOND = 4 * STEPS
 TILES = 8 * STEPS
 
 
-def kernel(x_hbm, wg_hbm, wu_hbm, wd_hbm, res_hbm, gain_ref, h_hbm, n_hbm, sum_in, x_buf, wg, wu, wd, hid, tiles, relay_in, sib_in, sum_out, sum_ld, res_ld, h_out, n_out,
-           x_sem, w_sem, relay_ssem, relay_rsem, sib_ssem, sib_rsem, sum_ssem, sum_rsem, ld_sem, res_sem, out_sem):
+def kernel(x_hbm, wg_hbm, wu_hbm, wd_hbm, res_hbm, gain_ref, h_ref, n_ref, sum_in, x_buf, wg, wu, wd, hid, tiles, relay_in, sib_in, sum_out, sum_last, sum_ld, res_ld,
+           x_sem, w_sem, relay_ssem, relay_rsem, sib_ssem, sib_rsem, sum_ssem, sum_rsem, ld_sem, res_sem):
     me = lax.axis_index("tp")
     c, cx, cy = me % 2, (me // 2) % 2, me // 4
     sib = cy * 4 + cx * 2 + (1 - c)
@@ -50,12 +52,18 @@
     def x_copy(i):
         return pltpu.make_async_copy(x_hbm.at[pl.ds(row_of(i), ROWS)], x_buf.at[i % 2], x_sem.at[i % 2])
 
-    def w_copies():
-        return [pltpu.make_async_copy(src, dst, w_sem.at[j]) for j, (src, dst) in enumerate(((wg_hbm, wg), (wu_hbm, wu), (wd_hbm, wd)))]
+    def w_copy(j, n):
+        src, dst = ((wg_hbm, wg), (wu_hbm, wu), (wd_hbm, wd))[j]
+        cols = pl.ds(n * COLS[j], COLS[j])
+        return pltpu.make_async_copy(src.at[:, cols], dst.at[:, cols], w_sem.at[j, n])
 
     x_copy(0).start()
-    for copy in w_copies():
-        copy.start()
+    for n in range(CHUNKS):
+        w_copy(0, n).start()
+        w_copy(1, n).start()
+    for n in range(CHUNKS):
+        w_copy(2, n).start()
+    x_copy(1).start()
 
     def relay_copy(i):
         via = (1 - c) * xn + c * yn + i % 2
@@ -73,29 +81,35 @@
             src_ref=tiles.at[RELAY_SLOTS + slot], dst_ref=sib_in.at[group, k], send_sem=sib_ssem.at[slot],
             recv_sem=sib_rsem.at[group, k], device_id={"tp": sib}, device_id_type=pl.DeviceIdType.MESH)
 
-    def sum_copy(direction, k, half):
+    def sum_copy(direction, k, half, in_vmem=False):
         slot = k % SUM_SLOTS
         to = (1 - direction) * xn + direction * yn + c
         return pltpu.make_async_remote_copy(
-            src_ref=sum_out.at[direction, slot, pl.ds(half * HALF, HALF)], dst_ref=sum_in.at[direction, k, half],
+            src_ref=sum_out.at[direction, slot, pl.ds(half * HALF, HALF)], dst_ref=sum_last.at[direction] if in_vmem else sum_in.at[direction, k, half],
             send_sem=sum_ssem.at[direction, slot, half], recv_sem=sum_rsem.at[direction, k, half],
             device_id={"tp": to}, device_id_type=pl.DeviceIdType.MESH)
 
-    def ffn(x_ref, out_ref):
-        for n in range(F // 256):
-            cols = slice(n * 256, (n + 1) * 256)
+    def ffn(x_ref, out_ref, loading=False):
+        for n in range(CHUNKS):
+            cols = slice(n * COLS[0], (n + 1) * COLS[0])
+            if loading:
+                w_copy(0, n).wait()
+                w_copy(1, n).wait()
             gate = jnp.dot(x_ref[...], wg[:, cols], preferred_element_type=jnp.float32)
             up = jnp.dot(x_ref[...], wu[:, cols], preferred_element_type=jnp.float32)
             hid[:, cols] = (gate * jax.nn.sigmoid(gate) * up).astype(jnp.bfloat16)
-        for n in range(D // 512):
-            cols = slice(n * 512, (n + 1) * 512)
+        for n in range(CHUNKS):
+            cols = slice(n * COLS[2], (n + 1) * COLS[2])
+            if loading:
+                w_copy(2, n).wait()
             out_ref[:, cols] = jnp.dot(hid[...], wd[:, cols], preferred_element_type=jnp.float32).astype(jnp.bfloat16)
 
-    for copy in w_copies():
-        copy.wait()
+    x_copy(0).wait()
+    ffn(x_buf.at[0], tiles.at[0], loading=True)
     pl.semaphore_wait(barrier, 5)
-
-    @pl.loop(0, TILES)
+    relay_copy(0).start()
+
+    @pl.loop(1, TILES)
     def _(i):
         first = 1 - (i + TILES - FIRST) // TILES
         last = (i + FIRST) // TILES
@@ -162,45 +176,54 @@
                     total = tiles[RELAY_SLOTS + 2, rows].astype(jnp.float32) + sib_in[direction, k_mid, rows].astype(jnp.float32)
                     sum_out[direction, k_mid % SUM_SLOTS, rows] = total + relay_in[direction, k_mid, rows].astype(jnp.float32)
 
-                sum_copy(direction, k_mid, half).start()
+                if half == 0:
+                    sum_copy(direction, k_mid, half).start()
+                else:
+                    @pl.when(k_mid < STEPS - 1)
+                    def _():
+                        sum_copy(direction, k_mid, 1).start()
+
+                    @pl.when(k_mid == STEPS - 1)
+                    def _():
+                        sum_copy(direction, k_mid, 1, in_vmem=True).start()
 
         @pl.when(is_final)
         def _():
             sib_copy(0, 2, k_last).wait_recv()
             pltpu.make_async_copy(res_hbm.at[pl.ds(0, ROWS)], res_ld, res_sem).wait()
-            for half in range(2):
-                for d in range(2):
-                    sum_copy(d, k_last, half).wait_recv()
-                loads = [pltpu.make_async_copy(sum_in.at[d, k_last, half], sum_ld.at[d], ld_sem.at[d]) for d in range(2)]
-                for load in loads:
-                    load.start()
-
-                def stores(k):
-                    rows = pl.ds(pl.multiple_of(k * ROWS + half * HALF, HALF), HALF)
-                    return [pltpu.make_async_copy(h_out.at[half], h_hbm.at[rows], out_sem.at[half, 0]),
-                            pltpu.make_async_copy(n_out.at[half], n_hbm.at[rows], out_sem.at[half, 1])]
-
-                @pl.when(k_last > 0)
-                def _():
-                    for store in stores(k_last - 1):
-                        store.wait()
-
-                for load in loads:
-                    load.wait()
-
+            def finish(half, sums):
                 @pl.loop(0, HALF // 16)
                 def _(b):
                     here = pl.ds(pl.multiple_of(b * 16, 16), 16)
                     rows = pl.ds(pl.multiple_of(half * HALF + b * 16, 16), 16)
+                    out = pl.ds(pl.multiple_of(k_last * ROWS + half * HALF + b * 16, 16), 16)
                     y_sum = tiles[RELAY_SLOTS + 2, rows].astype(jnp.float32) + sib_in[2, k_last, rows].astype(jnp.float32)
-                    y_sum = y_sum + (sum_ld[0, here] + sum_ld[1, here])
+                    y_sum = y_sum + (sums[0, here] + sums[1, here])
                     h = res_ld[rows].astype(jnp.float32) + y_sum
                     mean_sq = jnp.mean(h * h, axis=-1, keepdims=True)
-                    h_out[half, here] = h.astype(jnp.bfloat16)
-                    n_out[half, here] = (h * lax.rsqrt(mean_sq + EPS) * gain_ref[...]).astype(jnp.bfloat16)
-
-                for store in stores(k_last):
-                    store.start()
+                    h_ref[out] = h.astype(jnp.bfloat16)
+                    n_ref[out] = (h * lax.rsqrt(mean_sq + EPS) * gain_ref[...]).astype(jnp.bfloat16)
+
+            def finish_hbm(half):
+                loads = [pltpu.make_async_copy(sum_in.at[d, k_last, half], sum_ld.at[d], ld_sem.at[d]) for d in range(2)]
+                for d in range(2):
+                    sum_copy(d, k_last, half).wait_recv()
+                    loads[d].start()
+                for load in loads:
+                    load.wait()
+                finish(half, sum_ld)
+
+            finish_hbm(0)
+
+            @pl.when(k_last < STEPS - 1)
+            def _():
+                finish_hbm(1)
+
+            @pl.when(k_last == STEPS - 1)
+            def _():
+                for d in range(2):
+                    sum_copy(d, STEPS - 1, 1, in_vmem=True).wait_recv()
+                finish(1, sum_last)
 
     for s in range(RELAY_SLOTS):
         relay_copy(FIRST - RELAY_SLOTS + s).wait_send()
@@ -210,24 +233,32 @@
         for k in range(STEPS - SUM_SLOTS, STEPS):
             for half in range(2):
                 sum_copy(d, k, half).wait_send()
-    for half in range(2):
-        rows = pl.ds((STEPS - 1) * ROWS + half * HALF, HALF)
-        pltpu.make_async_copy(h_out.at[half], h_hbm.at[rows], out_sem.at[half, 0]).wait()
-        pltpu.make_async_copy(n_out.at[half], n_hbm.at[rows], out_sem.at[half, 1]).wait()
+
+def store_kernel(h_ref, n_ref, h_hbm, n_hbm, sem):
+    copies = []
+    for b in range(4):
+        rows = pl.ds(b * (BLOCK // 4), BLOCK // 4)
+        copies.append(pltpu.make_async_copy(h_ref.at[rows], h_hbm.at[rows], sem.at[0, b]))
+        copies.append(pltpu.make_async_copy(n_ref.at[rows], n_hbm.at[rows], sem.at[1, b]))
+    for copy in copies:
+        copy.start()
+    for copy in copies:
+        copy.wait()
 
 
 def solution(mesh):
     def local_block(x_in, w_gate, w_up, w_down, residual, norm_gain):
         hbm = pl.BlockSpec(memory_space=pltpu.HBM)
+        vmem = pl.BlockSpec(memory_space=pltpu.VMEM)
         h, n, _ = pl.pallas_call(
             kernel,
             out_shape=(
-                jax.ShapeDtypeStruct((BLOCK, D), jnp.bfloat16),
-                jax.ShapeDtypeStruct((BLOCK, D), jnp.bfloat16),
+                pltpu.VMEM((BLOCK, D), jnp.bfloat16),
+                pltpu.VMEM((BLOCK, D), jnp.bfloat16),
                 jax.ShapeDtypeStruct((2, STEPS, 2, HALF, D), jnp.float32),
             ),
-            in_specs=[hbm] * 5 + [pl.BlockSpec(memory_space=pltpu.VMEM)],
-            out_specs=(hbm, hbm, hbm),
+            in_specs=[hbm] * 5 + [vmem],
+            out_specs=(vmem, vmem, hbm),
             scratch_shapes=[
                 pltpu.VMEM((2, ROWS, D), jnp.bfloat16),
                 pltpu.VMEM((D, F), jnp.bfloat16),
@@ -239,11 +270,10 @@
                 pltpu.VMEM((3, STEPS, ROWS, D), jnp.bfloat16),
                 pltpu.VMEM((2, SUM_SLOTS, ROWS, D), jnp.float32),
                 pltpu.VMEM((2, HALF, D), jnp.float32),
+                pltpu.VMEM((2, HALF, D), jnp.float32),
                 pltpu.VMEM((ROWS, D), jnp.bfloat16),
-                pltpu.VMEM((2, HALF, D), jnp.bfloat16),
-                pltpu.VMEM((2, HALF, D), jnp.bfloat16),
                 pltpu.SemaphoreType.DMA((2,)),
-                pltpu.SemaphoreType.DMA((3,)),
+                pltpu.SemaphoreType.DMA((3, CHUNKS)),
                 pltpu.SemaphoreType.DMA((RELAY_SLOTS,)),
                 pltpu.SemaphoreType.DMA((2, STEPS)),
                 pltpu.SemaphoreType.DMA((2,)),
@@ -252,12 +282,19 @@
                 pltpu.SemaphoreType.DMA((2, STEPS, 2)),
                 pltpu.SemaphoreType.DMA((2,)),
                 pltpu.SemaphoreType.DMA,
-                pltpu.SemaphoreType.DMA((2, 2)),
             ],
-            compiler_params=pltpu.CompilerParams(collective_id=0, has_side_effects=True, vmem_limit_bytes=67000000),
+            compiler_params=pltpu.CompilerParams(collective_id=0, has_side_effects=True, vmem_limit_bytes=58000000),
             name="mlp_reduce",
         )(x_in, w_gate, w_up, w_down, residual, norm_gain.reshape(1, D))
-        return h, n
+        return pl.pallas_call(
+            store_kernel,
+            out_shape=(jax.ShapeDtypeStruct((BLOCK, D), jnp.bfloat16), jax.ShapeDtypeStruct((BLOCK, D), jnp.bfloat16)),
+            in_specs=[vmem, vmem],
+            out_specs=(hbm, hbm),
+            scratch_shapes=[pltpu.SemaphoreType.DMA((2, 4))],
+            compiler_params=pltpu.CompilerParams(vmem_limit_bytes=1048576),
+            name="store",
+        )(*(pltpu.with_memory_space_constraint(a, pltpu.VMEM) for a in (h, n)))
 
     row_spec = P(("data", "tp"), None)
     return jax.shard_map(local_block, mesh=mesh, in_specs=(P("data", None), P(None, "tp"), P(None, "tp"), P("tp", None), row_spec, P(None)), out_specs=(row_spec, row_spec), check_vma=False)

time: 296 us -> 291 us (0.983)
  local copies, waits for them, and re-layouts: 6.96 us -> 0 us
    unnamed x4 -> x0, local copies, waits for them, and re-layouts: 6.96 us -> none
    pallas_call x1 -> x2, Pallas kernels: 286 us -> 288 us  [the longest x1 284 us: local_block(): pl.pallas_call(kernel, out_shape=(pltpu.VMEM((BLOCK, D), jnp.bfloat16), p...]
where the time goes in v2:
time: 291 us; the launch traced here: 288 us
  Pallas kernels  288 us (99%)
    pallas_call x1, Pallas kernels, local_block(): pl.pallas_call(kernel, out_shape=(pltpu.VMEM((BLOCK, D), jnp.bfloat16), p...  284 us

profile of v2, /device:TPU:1, one launch (start us, length us, event | category | flops | bytes accessed | tf_op | source)
XLA Modules:
  0.0 288.5 jit_solution(1566643336078935402)
XLA Ops:
  0.6 284.5 %mlp_reduce.1 = (bf16[1024,2048]{1,0:T(8,128)(2,1)S(1)}, bf16[1024,2048]{1,0:T(8,128)(2,1)S(1)}, f32[2,4,2,128,2048]{4,3,2,1,0:T(8,128)}) custom-call(bf16[8192,2048]{1,0:T(8,128)(2,1)} %x_hbm.1, bf16[2048,1024]{1,0:T(8,128)(2,1)} %wg_hbm.1, bf16[2048,1024]{1,0:T(8,128)(2,1)} %wu_hbm.1, bf16[1024,2048]{1,0:T(8,128)(2,1)} %wd_hbm.1, ...), custom_call_target="tpu_custom_call" | custom-call | tf_op jit(solution)/shard_map/mlp_reduce/pallas_call | solution.py:253
  285.1 3.4 %store.1 = (bf16[1024,2048]{1,0:T(8,128)(2,1)}, bf16[1024,2048]{1,0:T(8,128)(2,1)}) custom-call(bf16[1024,2048]{1,0:T(8,128)(2,1)S(1)} %get-tuple-element.4.h_ref, bf16[1024,2048]{1,0:T(8,128)(2,1)S(1)} %get-tuple-element.5.n_ref), custom_call_target="tpu_custom_call" | custom-call | tf_op jit(solution)/shard_map/store/pallas_call | solution.py:289

commit v3 on v2

--- a/solution.py
+++ b/solution.py
@@ -66,10 +66,12 @@
     x_copy(1).start()
 
     def relay_copy(i):
-        via = (1 - c) * xn + c * yn + i % 2
+        k = i // 2
+        turn = (k + c) % 2
+        via = (1 - turn) * xn + turn * yn + i % 2
         return pltpu.make_async_remote_copy(
-            src_ref=tiles.at[i % RELAY_SLOTS], dst_ref=relay_in.at[1 - c, i // 2], send_sem=relay_ssem.at[i % RELAY_SLOTS],
-            recv_sem=relay_rsem.at[1 - c, i // 2], device_id={"tp": via}, device_id_type=pl.DeviceIdType.MESH)
+            src_ref=tiles.at[i % RELAY_SLOTS], dst_ref=relay_in.at[1 - turn, k], send_sem=relay_ssem.at[i % RELAY_SLOTS],
+            recv_sem=relay_rsem.at[1 - turn, k], device_id={"tp": via}, device_id_type=pl.DeviceIdType.MESH)
 
     def relay_arrival(group, k):
         return pltpu.make_async_remote_copy(

time: 291 us -> 290 us (level)
  no operation moved by 1% of the time
where the time goes in v3:
time: 290 us; the launch traced here: 289 us
  Pallas kernels  288 us (99%)
    pallas_call x1, Pallas kernels, local_block(): pl.pallas_call(kernel, out_shape=(pltpu.VMEM((BLOCK, D), jnp.bfloat16), p...  285 us

profile of v3, /device:TPU:1, one launch (start us, length us, event | category | flops | bytes accessed | tf_op | source)
XLA Modules:
  0.0 289.0 jit_solution(5145702668462395961)
XLA Ops:
  0.6 285.0 %mlp_reduce.1 = (bf16[1024,2048]{1,0:T(8,128)(2,1)S(1)}, bf16[1024,2048]{1,0:T(8,128)(2,1)S(1)}, f32[2,4,2,128,2048]{4,3,2,1,0:T(8,128)}) custom-call(bf16[8192,2048]{1,0:T(8,128)(2,1)} %x_hbm.1, bf16[2048,1024]{1,0:T(8,128)(2,1)} %wg_hbm.1, bf16[2048,1024]{1,0:T(8,128)(2,1)} %wu_hbm.1, bf16[1024,2048]{1,0:T(8,128)(2,1)} %wd_hbm.1, ...), custom_call_target="tpu_custom_call" | custom-call | tf_op jit(solution)/shard_map/mlp_reduce/pallas_call | solution.py:255
  285.7 3.4 %store.1 = (bf16[1024,2048]{1,0:T(8,128)(2,1)}, bf16[1024,2048]{1,0:T(8,128)(2,1)}) custom-call(bf16[1024,2048]{1,0:T(8,128)(2,1)S(1)} %get-tuple-element.4.h_ref, bf16[1024,2048]{1,0:T(8,128)(2,1)S(1)} %get-tuple-element.5.n_ref), custom_call_target="tpu_custom_call" | custom-call | tf_op jit(solution)/shard_map/store/pallas_call | solution.py:291

commit v4 on v2

--- a/solution.py
+++ b/solution.py
@@ -41,11 +41,11 @@
         mid = 1 - first - last
         p = i - FIRST
         q = p % 4
-        direction = q % 2
+        direction = (1 - c) + (q // 2) * (2 * c - 1)
         r = i - FIRST - SECOND
         ty = first * (1 - cy) + mid * (cy + direction * (1 - 2 * cy)) + last * cy
         tx = first * (1 - cx) + mid * (cx + (1 - direction) * (1 - 2 * cx)) + last * cx
-        tc = first * (i % 2) + mid * ((1 - c) + (q // 2) * (2 * c - 1)) + last * ((1 - c) + ((r + TILES) // STEPS - TILES // STEPS) * (2 * c - 1))
+        tc = first * (i % 2) + mid * (q % 2) + last * ((1 - c) + ((r + TILES) // STEPS - TILES // STEPS) * (2 * c - 1))
         k = first * (i // 2) + mid * (p // 4) + last * (i % STEPS)
         return pl.multiple_of((ty * 4 + tx * 2 + tc) * BLOCK + k * ROWS, ROWS)
 
@@ -65,29 +65,30 @@
         w_copy(2, n).start()
     x_copy(1).start()
 
+    out_chip = (1 - c) * xn + c * yn
+
     def relay_copy(i):
-        via = (1 - c) * xn + c * yn + i % 2
         return pltpu.make_async_remote_copy(
-            src_ref=tiles.at[i % RELAY_SLOTS], dst_ref=relay_in.at[1 - c, i // 2], send_sem=relay_ssem.at[i % RELAY_SLOTS],
-            recv_sem=relay_rsem.at[1 - c, i // 2], device_id={"tp": via}, device_id_type=pl.DeviceIdType.MESH)
-
-    def relay_arrival(group, k):
-        return pltpu.make_async_remote_copy(
-            src_ref=relay_in.at[group, k], dst_ref=relay_in.at[group, k], send_sem=relay_ssem.at[0],
-            recv_sem=relay_rsem.at[group, k], device_id={"tp": sib}, device_id_type=pl.DeviceIdType.MESH)
+            src_ref=tiles.at[i % RELAY_SLOTS], dst_ref=relay_in.at[i % 2, i // 2], send_sem=relay_ssem.at[i % RELAY_SLOTS],
+            recv_sem=relay_rsem.at[i % 2, i // 2], device_id={"tp": out_chip + 1 - c}, device_id_type=pl.DeviceIdType.MESH)
 
     def sib_copy(slot, group, k):
         return pltpu.make_async_remote_copy(
             src_ref=tiles.at[RELAY_SLOTS + slot], dst_ref=sib_in.at[group, k], send_sem=sib_ssem.at[slot],
             recv_sem=sib_rsem.at[group, k], device_id={"tp": sib}, device_id_type=pl.DeviceIdType.MESH)
 
-    def sum_copy(direction, k, half, in_vmem=False):
+    def sum_copy(j, k, half, in_vmem=False):
         slot = k % SUM_SLOTS
-        to = (1 - direction) * xn + direction * yn + c
         return pltpu.make_async_remote_copy(
-            src_ref=sum_out.at[direction, slot, pl.ds(half * HALF, HALF)], dst_ref=sum_last.at[direction] if in_vmem else sum_in.at[direction, k, half],
-            send_sem=sum_ssem.at[direction, slot, half], recv_sem=sum_rsem.at[direction, k, half],
-            device_id={"tp": to}, device_id_type=pl.DeviceIdType.MESH)
+            src_ref=sum_out.at[j, slot, pl.ds(half * HALF, HALF)], dst_ref=sum_last.at[c] if in_vmem else sum_in.at[c, k, half],
+            send_sem=sum_ssem.at[j, slot, half], recv_sem=sum_rsem.at[c, k, half],
+            device_id={"tp": out_chip + j}, device_id_type=pl.DeviceIdType.MESH)
+
+    def sum_arrival(d, k, half, in_vmem=False):
+        here = sum_last.at[d] if in_vmem else sum_in.at[d, k, half]
+        return pltpu.make_async_remote_copy(
+            src_ref=here, dst_ref=here, send_sem=sum_ssem.at[0, 0, 0], recv_sem=sum_rsem.at[d, k, half],
+            device_id={"tp": sib}, device_id_type=pl.DeviceIdType.MESH)
 
     def ffn(x_ref, out_ref, loading=False):
         for n in range(CHUNKS):
@@ -116,7 +117,7 @@
         mid = 1 - first - last
         p = i - FIRST
         q = p % 4
-        direction = q % 2
+        j = q % 2
         k_mid = p // 4
         k_last = i % STEPS
         is_relay = i < FIRST
@@ -153,7 +154,7 @@
 
         @pl.when(is_sib)
         def _():
-            sib_copy(i % 2, direction, k_mid).start()
+            sib_copy(i % 2, j, k_mid).start()
 
         @pl.when(is_own_sib)
         def _():
@@ -161,31 +162,31 @@
 
         @pl.when(is_sum)
         def _():
-            sib_copy(0, direction, k_mid).wait_recv()
-            relay_arrival(direction, k_mid).wait_recv()
+            sib_copy(0, j, k_mid).wait_recv()
+            relay_copy(2 * k_mid + j).wait_recv()
 
             @pl.when(k_mid >= SUM_SLOTS)
             def _():
                 for half in range(2):
-                    sum_copy(direction, k_mid - SUM_SLOTS, half).wait_send()
+                    sum_copy(j, k_mid - SUM_SLOTS, half).wait_send()
 
             for half in range(2):
                 @pl.loop(0, HALF // 16)
                 def _(b):
                     rows = pl.ds(pl.multiple_of(half * HALF + b * 16, 16), 16)
-                    total = tiles[RELAY_SLOTS + 2, rows].astype(jnp.float32) + sib_in[direction, k_mid, rows].astype(jnp.float32)
-                    sum_out[direction, k_mid % SUM_SLOTS, rows] = total + relay_in[direction, k_mid, rows].astype(jnp.float32)
+                    total = tiles[RELAY_SLOTS + 2, rows].astype(jnp.float32) + sib_in[j, k_mid, rows].astype(jnp.float32)
+                    sum_out[j, k_mid % SUM_SLOTS, rows] = total + relay_in[j, k_mid, rows].astype(jnp.float32)
 
                 if half == 0:
-                    sum_copy(direction, k_mid, half).start()
+                    sum_copy(j, k_mid, half).start()
                 else:
                     @pl.when(k_mid < STEPS - 1)
                     def _():
-                        sum_copy(direction, k_mid, 1).start()
+                        sum_copy(j, k_mid, 1).start()
 
                     @pl.when(k_mid == STEPS - 1)
                     def _():
-                        sum_copy(direction, k_mid, 1, in_vmem=True).start()
+                        sum_copy(j, k_mid, 1, in_vmem=True).start()
 
         @pl.when(is_final)
         def _():
@@ -207,7 +208,7 @@
             def finish_hbm(half):
                 loads = [pltpu.make_async_copy(sum_in.at[d, k_last, half], sum_ld.at[d], ld_sem.at[d]) for d in range(2)]
                 for d in range(2):
-                    sum_copy(d, k_last, half).wait_recv()
+                    sum_arrival(d, k_last, half).wait_recv()
                     loads[d].start()
                 for load in loads:
                     load.wait()
@@ -222,7 +223,7 @@
             @pl.when(k_last == STEPS - 1)
             def _():
                 for d in range(2):
-                    sum_copy(d, STEPS - 1, 1, in_vmem=True).wait_recv()
+                    sum_arrival(d, STEPS - 1, 1, in_vmem=True).wait_recv()
                 finish(1, sum_last)
 
     for s in range(RELAY_SLOTS):

time: 291 us -> 289 us (level)
  no operation moved by 1% of the time
where the time goes in v4:
time: 289 us
  Pallas kernels  288 us (100%)
    pallas_call x1, Pallas kernels, local_block(): pl.pallas_call(kernel, out_shape=(pltpu.VMEM((BLOCK, D), jnp.bfloat16), p...  285 us

profile of v4, /device:TPU:1, one launch (start us, length us, event | category | flops | bytes accessed | tf_op | source)
XLA Modules:
  0.0 289.0 jit_solution(2335995672661702169)
XLA Ops:
  0.6 285.0 %mlp_reduce.1 = (bf16[1024,2048]{1,0:T(8,128)(2,1)S(1)}, bf16[1024,2048]{1,0:T(8,128)(2,1)S(1)}, f32[2,4,2,128,2048]{4,3,2,1,0:T(8,128)}) custom-call(bf16[8192,2048]{1,0:T(8,128)(2,1)} %x_hbm.1, bf16[2048,1024]{1,0:T(8,128)(2,1)} %wg_hbm.1, bf16[2048,1024]{1,0:T(8,128)(2,1)} %wu_hbm.1, bf16[1024,2048]{1,0:T(8,128)(2,1)} %wd_hbm.1, ...), custom_call_target="tpu_custom_call" | custom-call | tf_op jit(solution)/shard_map/mlp_reduce/pallas_call | solution.py:254
  285.7 3.4 %store.1 = (bf16[1024,2048]{1,0:T(8,128)(2,1)}, bf16[1024,2048]{1,0:T(8,128)(2,1)}) custom-call(bf16[1024,2048]{1,0:T(8,128)(2,1)S(1)} %get-tuple-element.4.h_ref, bf16[1024,2048]{1,0:T(8,128)(2,1)S(1)} %get-tuple-element.5.n_ref), custom_call_target="tpu_custom_call" | custom-call | tf_op jit(solution)/shard_map/store/pallas_call | solution.py:290

commit v5 on v4

v5 whole, which is shorter than its diff:
```python
import functools

import jax
import jax.numpy as jnp
from jax import lax
from jax.experimental import pallas as pl
from jax.experimental.pallas import tpu as pltpu
from jax.sharding import PartitionSpec as P

EPS = 1e-5
ROWS = 256
CHUNKS = 4
COLS = (256, 256, 512)
HALF = 128
BLOCK = 1024
STEPS = BLOCK // ROWS
D = 2048
F = 1024
HID_SLOTS = 6
SUM_SLOTS = 2
FIRST = 2 * STEPS
SECOND = FIRST + STEPS
THIRD = SECOND + 4 * STEPS
TILES = 8 * STEPS


def kernel(x_hbm, wg_hbm, wu_hbm, wd_hbm, res_hbm, gain_ref, h_ref, n_ref, sum_in, x_buf, wg, wu, wd, wd_relay, hid, tiles, hid_in, sib_in, sum_out, sum_last, sum_ld, res_ld,
           x_sem, w_sem, wr_sem, relay_ssem, relay_rsem, sib_ssem, sib_rsem, sum_ssem, sum_rsem, ld_sem, res_sem):
    me = lax.axis_index("tp")
    c, cx, cy = me % 2, (me // 2) % 2, me // 4
    sib = cy * 4 + cx * 2 + (1 - c)
    xn = cy * 4 + (1 - cx) * 2
    yn = (1 - cy) * 4 + cx * 2

    barrier = pltpu.get_barrier_semaphore()
    for dev in (sib, xn, xn + 1, yn, yn + 1):
        pl.semaphore_signal(barrier, inc=1, device_id={"tp": dev}, device_id_type=pl.DeviceIdType.MESH)

    def kinds(i):
        past_first, past_second, past_third = (i + TILES - FIRST) // TILES, (i + TILES - SECOND) // TILES, (i + TILES - THIRD) // TILES
        return 1 - past_first, past_first - past_second, past_second - past_third, past_third

    def row_of(i):
        diag, to_sib, to_chip, kept = kinds(i)
        q = i % 4
        direction = (1 - c) + (q // 2) * (2 * c - 1)
        ty = diag * (1 - cy) + to_chip * (cy + direction * (1 - 2 * cy)) + (to_sib + kept) * cy
        tx = diag * (1 - cx) + to_chip * (cx + (1 - direction) * (1 - 2 * cx)) + (to_sib + kept) * cx
        tc = (diag + to_chip) * (i % 2) + to_sib * (1 - c) + kept * c
        k = diag * (i // 2) + to_chip * ((i - SECOND) // 4) + (to_sib + kept) * (i % STEPS)
        return pl.multiple_of((ty * 4 + tx * 2 + tc) * BLOCK + k * ROWS, ROWS)

    def x_copy(i):
        return pltpu.make_async_copy(x_hbm.at[pl.ds(row_of(i), ROWS)], x_buf.at[i % 2], x_sem.at[i % 2])

    def w_copy(j, n):
        src, dst = ((wg_hbm, wg), (wu_hbm, wu), (wd_hbm, wd))[j]
        cols = pl.ds(n * COLS[j], COLS[j])
        return pltpu.make_async_copy(src.at[:, cols], dst.at[:, cols], w_sem.at[j, n])

    x_copy(0).start()
    for n in range(CHUNKS):
        w_copy(0, n).start()
        w_copy(1, n).start()
    for n in range(CHUNKS):
        w_copy(2, n).start()
    x_copy(1).start()

    out_chip = (1 - c) * xn + c * yn

    def w_relay_copy():
        return pltpu.make_async_remote_copy(
            src_ref=wd_hbm, dst_ref=wd_relay, send_sem=wr_sem.at[0], recv_sem=wr_sem.at[1],
            device_id={"tp": out_chip + 1 - c}, device_id_type=pl.DeviceIdType.MESH)

    def relay_copy(i):
        return pltpu.make_async_remote_copy(
            src_ref=hid.at[i % HID_SLOTS], dst_ref=hid_in.at[i % 2, i // 2], send_sem=relay_ssem.at[i % HID_SLOTS],
            recv_sem=relay_rsem.at[i % 2, i // 2], device_id={"tp": out_chip + 1 - c}, device_id_type=pl.DeviceIdType.MESH)

    def sib_copy(slot, group, k):
        return pltpu.make_async_remote_copy(
            src_ref=tiles.at[slot], dst_ref=sib_in.at[group, k], send_sem=sib_ssem.at[slot],
            recv_sem=sib_rsem.at[group, k], device_id={"tp": sib}, device_id_type=pl.DeviceIdType.MESH)

    def sum_copy(j, k, half, in_vmem=False):
        slot = k % SUM_SLOTS
        return pltpu.make_async_remote_copy(
            src_ref=sum_out.at[j, slot, pl.ds(half * HALF, HALF)], dst_ref=sum_last.at[c] if in_vmem else sum_in.at[c, k, half],
            send_sem=sum_ssem.at[j, slot, half], recv_sem=sum_rsem.at[c, k, half],
            device_id={"tp": out_chip + j}, device_id_type=pl.DeviceIdType.MESH)

    def sum_arrival(d, k, half, in_vmem=False):
        here = sum_last.at[d] if in_vmem else sum_in.at[d, k, half]
        return pltpu.make_async_remote_copy(
            src_ref=here, dst_ref=here, send_sem=sum_ssem.at[0, 0, 0], recv_sem=sum_rsem.at[d, k, half],
            device_id={"tp": sib}, device_id_type=pl.DeviceIdType.MESH)

    def gate_up(x_ref, out_ref, loading=False):
        for n in range(CHUNKS):
            cols = slice(n * COLS[0], (n + 1) * COLS[0])
            if loading:
                w_copy(0, n).wait()
                w_copy(1, n).wait()
            gate = jnp.dot(x_ref[...], wg[:, cols], preferred_element_type=jnp.float32)
            up = jnp.dot(x_ref[...], wu[:, cols], preferred_element_type=jnp.float32)
            out_ref[:, cols] = (gate * jax.nn.sigmoid(gate) * up).astype(jnp.bfloat16)

    pl.semaphore_wait(barrier, 5)
    w_relay_copy().start()
    x_copy(0).wait()
    gate_up(x_buf.at[0], hid.at[0], loading=True)
    relay_copy(0).start()
    for n in range(CHUNKS):
        w_copy(2, n).wait()

    @pl.loop(1, TILES)
    def _(i):
        diag, to_sib, to_chip, kept = kinds(i)
        j = i % 2
        k_chip = (i - SECOND) // 4
        k_own = i % STEPS
        stays = to_chip * (i % 4 // 2) + kept
        is_relay = i < FIRST
        in_chip = jnp.logical_and(i >= SECOND, i < THIRD)
        is_own_sib = jnp.logical_and(i >= FIRST, i < SECOND)
        is_sib = jnp.logical_and(in_chip, i % 4 < 2)
        is_sum = jnp.logical_and(in_chip, i % 4 >= 2)
        is_final = i >= THIRD

        @pl.when(i + 1 < TILES)
        def _():
            x_copy(i + 1).start()

        x_copy(i).wait()

        @pl.when(jnp.logical_and(is_relay, i >= HID_SLOTS))
        def _():
            relay_copy(i - HID_SLOTS).wait_send()

        @pl.when(jnp.logical_and(jnp.logical_or(is_sib, is_own_sib), i >= FIRST + 2))
        def _():
            sib_copy(j, 0, 0).wait_send()

        @pl.when(is_final)
        def _():
            pltpu.make_async_copy(res_hbm.at[pl.ds(pl.multiple_of(k_own * ROWS, ROWS), ROWS)], res_ld, res_sem).start()

        hid_slot = diag * (i % HID_SLOTS) + (1 - diag) * HID_SLOTS
        gate_up(x_buf.at[i % 2], hid.at[hid_slot])

        @pl.when(is_relay)
        def _():
            relay_copy(i).start()

        @pl.when(i >= FIRST)
        def _():
            slot = stays * 2 + (1 - stays) * j
            for n in range(CHUNKS):
                cols = slice(n * COLS[2], (n + 1) * COLS[2])
                tiles[slot, :, cols] = jnp.dot(hid[HID_SLOTS], wd[:, cols], preferred_element_type=jnp.float32).astype(jnp.bfloat16)

        @pl.when(is_sib)
        def _():
            sib_copy(j, j, k_chip).start()

        @pl.when(is_own_sib)
        def _():
            sib_copy(j, 2, k_own).start()

        @pl.when(is_sum)
        def _():
            sib_copy(0, j, k_chip).wait_recv()
            relay_copy(2 * k_chip + j).wait_recv()

            @pl.when(i == SECOND + 2)
            def _():
                w_relay_copy().wait_recv()

            @pl.when(k_chip >= SUM_SLOTS)
            def _():
                for half in range(2):
                    sum_copy(j, k_chip - SUM_SLOTS, half).wait_send()

            for n in range(CHUNKS):
                cols = slice(n * COLS[2], (n + 1) * COLS[2])
                relayed = jnp.dot(hid_in[j, k_chip], wd_relay[:, cols], preferred_element_type=jnp.float32).astype(jnp.bfloat16)
                total = tiles[2, :, cols].astype(jnp.float32) + sib_in[j, k_chip, :, cols].astype(jnp.float32)
                sum_out[j, k_chip % SUM_SLOTS, :, cols] = total + relayed.astype(jnp.float32)

            sum_copy(j, k_chip, 0).start()

            @pl.when(k_chip < STEPS - 1)
            def _():
                sum_copy(j, k_chip, 1).start()

            @pl.when(k_chip == STEPS - 1)
            def _():
                sum_copy(j, k_chip, 1, in_vmem=True).start()

        @pl.when(is_final)
        def _():
            sib_copy(0, 2, k_own).wait_recv()
            pltpu.make_async_copy(res_hbm.at[pl.ds(0, ROWS)], res_ld, res_sem).wait()
            def finish(half, sums):
                @pl.loop(0, HALF // 16)
                def _(b):
                    here = pl.ds(pl.multiple_of(b * 16, 16), 16)
                    rows = pl.ds(pl.multiple_of(half * HALF + b * 16, 16), 16)
                    out = pl.ds(pl.multiple_of(k_own * ROWS + half * HALF + b * 16, 16), 16)
                    y_sum = tiles[2, rows].astype(jnp.float32) + sib_in[2, k_own, rows].astype(jnp.float32)
                    y_sum = y_sum + (sums[0, here] + sums[1, here])
                    h = res_ld[rows].astype(jnp.float32) + y_sum
                    mean_sq = jnp.mean(h * h, axis=-1, keepdims=True)
                    h_ref[out] = h.astype(jnp.bfloat16)
                    n_ref[out] = (h * lax.rsqrt(mean_sq + EPS) * gain_ref[...]).astype(jnp.bfloat16)

            def finish_hbm(half):
                loads = [pltpu.make_async_copy(sum_in.at[d, k_own, half], sum_ld.at[d], ld_sem.at[d]) for d in range(2)]
                for d in range(2):
                    sum_arrival(d, k_own, half).wait_recv()
                    loads[d].start()
                for load in loads:
                    load.wait()
                finish(half, sum_ld)

            finish_hbm(0)

            @pl.when(k_own < STEPS - 1)
            def _():
                finish_hbm(1)

            @pl.when(k_own == STEPS - 1)
            def _():
                for d in range(2):
                    sum_arrival(d, STEPS - 1, 1, in_vmem=True).wait_recv()
                finish(1, sum_last)

    w_relay_copy().wait_send()
    for s in range(HID_SLOTS):
        relay_copy(FIRST - HID_SLOTS + s).wait_send()
    for s in range(2):
        sib_copy(s, 0, 0).wait_send()
    for d in range(2):
        for k in range(STEPS - SUM_SLOTS, STEPS):
            for half in range(2):
                sum_copy(d, k, half).wait_send()

def store_kernel(h_ref, n_ref, h_hbm, n_hbm, sem):
    copies = []
    for b in range(4):
        rows = pl.ds(b * (BLOCK // 4), BLOCK // 4)
        copies.append(pltpu.make_async_copy(h_ref.at[rows], h_hbm.at[rows], sem.at[0, b]))
        copies.append(pltpu.make_async_copy(n_ref.at[rows], n_hbm.at[rows], sem.at[1, b]))
    for copy in copies:
        copy.start()
    for copy in copies:
        copy.wait()


def solution(mesh):
    def local_block(x_in, w_gate, w_up, w_down, residual, norm_gain):
        hbm = pl.BlockSpec(memory_space=pltpu.HBM)
        vmem = pl.BlockSpec(memory_space=pltpu.VMEM)
        h, n, _ = pl.pallas_call(
            kernel,
            out_shape=(
                pltpu.VMEM((BLOCK, D), jnp.bfloat16),
                pltpu.VMEM((BLOCK, D), jnp.bfloat16),
                jax.ShapeDtypeStruct((2, STEPS, 2, HALF, D), jnp.float32),
            ),
            in_specs=[hbm] * 5 + [vmem],
            out_specs=(vmem, vmem, hbm),
            scratch_shapes=[
                pltpu.VMEM((2, ROWS, D), jnp.bfloat16),
                pltpu.VMEM((D, F), jnp.bfloat16),
                pltpu.VMEM((D, F), jnp.bfloat16),
                pltpu.VMEM((F, D), jnp.bfloat16),
                pltpu.VMEM((F, D), jnp.bfloat16),
                pltpu.VMEM((HID_SLOTS + 1, ROWS, F), jnp.bfloat16),
                pltpu.VMEM((3, ROWS, D), jnp.bfloat16),
                pltpu.VMEM((2, STEPS, ROWS, F), jnp.bfloat16),
                pltpu.VMEM((3, STEPS, ROWS, D), jnp.bfloat16),
                pltpu.VMEM((2, SUM_SLOTS, ROWS, D), jnp.float32),
                pltpu.VMEM((2, HALF, D), jnp.float32),
                pltpu.VMEM((2, HALF, D), jnp.float32),
                pltpu.VMEM((ROWS, D), jnp.bfloat16),
                pltpu.SemaphoreType.DMA((2,)),
                pltpu.SemaphoreType.DMA((3, CHUNKS)),
                pltpu.SemaphoreType.DMA((2,)),
                pltpu.SemaphoreType.DMA((HID_SLOTS,)),
                pltpu.SemaphoreType.DMA((2, STEPS)),
                pltpu.SemaphoreType.DMA((2,)),
                pltpu.SemaphoreType.DMA((3, STEPS)),
                pltpu.SemaphoreType.DMA((2, SUM_SLOTS, 2)),
                pltpu.SemaphoreType.DMA((2, STEPS, 2)),
                pltpu.SemaphoreType.DMA((2,)),
                pltpu.SemaphoreType.DMA,
            ],
            compiler_params=pltpu.CompilerParams(collective_id=0, has_side_effects=True, vmem_limit_bytes=58000000),
            name="mlp_reduce",
        )(x_in, w_gate, w_up, w_down, residual, norm_gain.reshape(1, D))
        return pl.pallas_call(
            store_kernel,
            out_shape=(jax.ShapeDtypeStruct((BLOCK, D), jnp.bfloat16), jax.ShapeDtypeStruct((BLOCK, D), jnp.bfloat16)),
            in_specs=[vmem, vmem],
            out_specs=(hbm, hbm),
            scratch_shapes=[pltpu.SemaphoreType.DMA((2, 4))],
            compiler_params=pltpu.CompilerParams(vmem_limit_bytes=1048576),
            name="store",
        )(*(pltpu.with_memory_space_constraint(a, pltpu.VMEM) for a in (h, n)))

    row_spec = P(("data", "tp"), None)
    return jax.shard_map(local_block, mesh=mesh, in_specs=(P("data", None), P(None, "tp"), P(None, "tp"), P("tp", None), row_spec, P(None)), out_specs=(row_spec, row_spec), check_vma=False)
```

time: 289 us -> 282 us (0.976)
  Pallas kernels: 288 us -> 281 us
    pallas_call x1, Pallas kernels: 285 us -> 277 us  [local_block(): pl.pallas_call(kernel, out_shape=(pltpu.VMEM((BLOCK, D), jnp.bfloat16), p...]
where the time goes in v5:
time: 282 us; the launch traced here: 281 us
  Pallas kernels  281 us (100%)
    pallas_call x1, Pallas kernels, local_block(): pl.pallas_call(kernel, out_shape=(pltpu.VMEM((BLOCK, D), jnp.bfloat16), p...  277 us

profile of v5, /device:TPU:1, one launch (start us, length us, event | category | flops | bytes accessed | tf_op | source)
XLA Modules:
  0.0 281.5 jit_solution(3938085895215896162)
XLA Ops:
  0.6 277.5 %mlp_reduce.1 = (bf16[1024,2048]{1,0:T(8,128)(2,1)S(1)}, bf16[1024,2048]{1,0:T(8,128)(2,1)S(1)}, f32[2,4,2,128,2048]{4,3,2,1,0:T(8,128)}) custom-call(bf16[8192,2048]{1,0:T(8,128)(2,1)} %x_hbm.1, bf16[2048,1024]{1,0:T(8,128)(2,1)} %wg_hbm.1, bf16[2048,1024]{1,0:T(8,128)(2,1)} %wu_hbm.1, bf16[1024,2048]{1,0:T(8,128)(2,1)} %wd_hbm.1, ...), custom_call_target="tpu_custom_call" | custom-call | tf_op jit(solution)/shard_map/mlp_reduce/pallas_call | solution.py:265
  278.1 3.4 %store.1 = (bf16[1024,2048]{1,0:T(8,128)(2,1)}, bf16[1024,2048]{1,0:T(8,128)(2,1)}) custom-call(bf16[1024,2048]{1,0:T(8,128)(2,1)S(1)} %get-tuple-element.4.h_ref, bf16[1024,2048]{1,0:T(8,128)(2,1)S(1)} %get-tuple-element.5.n_ref), custom_call_target="tpu_custom_call" | custom-call | tf_op jit(solution)/shard_map/store/pallas_call | solution.py:303

commit v6 on v5

--- a/solution.py
+++ b/solution.py
@@ -12,6 +12,7 @@
 CHUNKS = 4
 COLS = (256, 256, 512)
 HALF = 128
+LATE = 32
 BLOCK = 1024
 STEPS = BLOCK // ROWS
 D = 2048
@@ -24,8 +25,8 @@
 TILES = 8 * STEPS
 
 
-def kernel(x_hbm, wg_hbm, wu_hbm, wd_hbm, res_hbm, gain_ref, h_ref, n_ref, sum_in, x_buf, wg, wu, wd, wd_relay, hid, tiles, hid_in, sib_in, sum_out, sum_last, sum_ld, res_ld,
-           x_sem, w_sem, wr_sem, relay_ssem, relay_rsem, sib_ssem, sib_rsem, sum_ssem, sum_rsem, ld_sem, res_sem):
+def kernel(x_hbm, wg_hbm, wu_hbm, wd_hbm, res_hbm, gain_hbm, h_ref, n_ref, sum_in, x_buf, wg, wu, wd, wd_relay, hid, tiles, hid_in, sib_in, sum_out, sum_last, sum_ld, res_ld, gain_ref,
+           x_sem, w_sem, wr_sem, relay_ssem, relay_rsem, sib_ssem, sib_rsem, sum_ssem, sum_rsem, ld_sem, res_sem, gain_sem):
     me = lax.axis_index("tp")
     c, cx, cy = me % 2, (me // 2) % 2, me // 4
     sib = cy * 4 + cx * 2 + (1 - c)
@@ -33,7 +34,7 @@
     yn = (1 - cy) * 4 + cx * 2
 
     barrier = pltpu.get_barrier_semaphore()
-    for dev in (sib, xn, xn + 1, yn, yn + 1):
+    for dev in (sib, (1 - c) * (yn + 1) + c * xn, (1 - c) * xn + c * (yn + 1)):
         pl.semaphore_signal(barrier, inc=1, device_id={"tp": dev}, device_id_type=pl.DeviceIdType.MESH)
 
     def kinds(i):
@@ -65,6 +66,8 @@
     for n in range(CHUNKS):
         w_copy(2, n).start()
     x_copy(1).start()
+    gain_copy = pltpu.make_async_copy(gain_hbm, gain_ref, gain_sem)
+    gain_copy.start()
 
     out_chip = (1 - c) * xn + c * yn
 
@@ -83,17 +86,24 @@
             src_ref=tiles.at[slot], dst_ref=sib_in.at[group, k], send_sem=sib_ssem.at[slot],
             recv_sem=sib_rsem.at[group, k], device_id={"tp": sib}, device_id_type=pl.DeviceIdType.MESH)
 
-    def sum_copy(j, k, half, in_vmem=False):
+    def piece(part):
+        return (pl.ds(0, HALF), pl.ds(HALF, HALF), pl.ds(HALF, HALF - LATE), pl.ds(ROWS - LATE, LATE))[part]
+
+    def landing(d, k, part):
+        if part < 2:
+            return sum_in.at[d, k, part]
+        return sum_last.at[d, pl.ds(0, HALF - LATE) if part == 2 else pl.ds(HALF - LATE, LATE)]
+
+    def sum_copy(j, k, part):
         slot = k % SUM_SLOTS
         return pltpu.make_async_remote_copy(
-            src_ref=sum_out.at[j, slot, pl.ds(half * HALF, HALF)], dst_ref=sum_last.at[c] if in_vmem else sum_in.at[c, k, half],
-            send_sem=sum_ssem.at[j, slot, half], recv_sem=sum_rsem.at[c, k, half],
+            src_ref=sum_out.at[j, slot, piece(part)], dst_ref=landing(c, k, part),
+            send_sem=sum_ssem.at[j, slot, part], recv_sem=sum_rsem.at[c, k, part],
             device_id={"tp": out_chip + j}, device_id_type=pl.DeviceIdType.MESH)
 
-    def sum_arrival(d, k, half, in_vmem=False):
-        here = sum_last.at[d] if in_vmem else sum_in.at[d, k, half]
-        return pltpu.make_async_remote_copy(
-            src_ref=here, dst_ref=here, send_sem=sum_ssem.at[0, 0, 0], recv_sem=sum_rsem.at[d, k, half],
+    def sum_arrival(d, k, part):
+        return pltpu.make_async_remote_copy(
+            src_ref=landing(d, k, part), dst_ref=landing(d, k, part), send_sem=sum_ssem.at[0, 0, 0], recv_sem=sum_rsem.at[d, k, part],
             device_id={"tp": sib}, device_id_type=pl.DeviceIdType.MESH)
 
     def gate_up(x_ref, out_ref, loading=False):
@@ -106,13 +116,14 @@
             up = jnp.dot(x_ref[...], wu[:, cols], preferred_element_type=jnp.float32)
             out_ref[:, cols] = (gate * jax.nn.sigmoid(gate) * up).astype(jnp.bfloat16)
 
-    pl.semaphore_wait(barrier, 5)
+    pl.semaphore_wait(barrier, 3)
     w_relay_copy().start()
     x_copy(0).wait()
     gate_up(x_buf.at[0], hid.at[0], loading=True)
     relay_copy(0).start()
     for n in range(CHUNKS):
         w_copy(2, n).wait()
+    gain_copy.wait()
 
     @pl.loop(1, TILES)
     def _(i):
@@ -196,21 +207,22 @@
 
             @pl.when(k_chip == STEPS - 1)
             def _():
-                sum_copy(j, k_chip, 1, in_vmem=True).start()
+                for part in (2, 3):
+                    sum_copy(j, k_chip, part).start()
 
         @pl.when(is_final)
         def _():
             sib_copy(0, 2, k_own).wait_recv()
             pltpu.make_async_copy(res_hbm.at[pl.ds(0, ROWS)], res_ld, res_sem).wait()
-            def finish(half, sums):
-                @pl.loop(0, HALF // 16)
+            def finish(start, rows, sums, sums_start):
+                @pl.loop(0, rows // 16)
                 def _(b):
-                    here = pl.ds(pl.multiple_of(b * 16, 16), 16)
-                    rows = pl.ds(pl.multiple_of(half * HALF + b * 16, 16), 16)
-                    out = pl.ds(pl.multiple_of(k_own * ROWS + half * HALF + b * 16, 16), 16)
-                    y_sum = tiles[2, rows].astype(jnp.float32) + sib_in[2, k_own, rows].astype(jnp.float32)
+                    here = pl.ds(pl.multiple_of(sums_start + b * 16, 16), 16)
+                    tile = pl.ds(pl.multiple_of(start + b * 16, 16), 16)
+                    out = pl.ds(pl.multiple_of(k_own * ROWS + start + b * 16, 16), 16)
+                    y_sum = tiles[2, tile].astype(jnp.float32) + sib_in[2, k_own, tile].astype(jnp.float32)
                     y_sum = y_sum + (sums[0, here] + sums[1, here])
-                    h = res_ld[rows].astype(jnp.float32) + y_sum
+                    h = res_ld[tile].astype(jnp.float32) + y_sum
                     mean_sq = jnp.mean(h * h, axis=-1, keepdims=True)
                     h_ref[out] = h.astype(jnp.bfloat16)
                     n_ref[out] = (h * lax.rsqrt(mean_sq + EPS) * gain_ref[...]).astype(jnp.bfloat16)
@@ -222,7 +234,7 @@
                     loads[d].start()
                 for load in loads:
                     load.wait()
-                finish(half, sum_ld)
+                finish(half * HALF, HALF, sum_ld, 0)
 
             finish_hbm(0)
 
@@ -232,19 +244,22 @@
 
             @pl.when(k_own == STEPS - 1)
             def _():
-                for d in range(2):
-                    sum_arrival(d, STEPS - 1, 1, in_vmem=True).wait_recv()
-                finish(1, sum_last)
+                for part, rows in ((2, HALF - LATE), (3, LATE)):
+                    for d in range(2):
+                        sum_arrival(d, STEPS - 1, part).wait_recv()
+                    start = (part - 2) * (HALF - LATE)
+                    finish(HALF + start, rows, sum_last, start)
 
     w_relay_copy().wait_send()
     for s in range(HID_SLOTS):
         relay_copy(FIRST - HID_SLOTS + s).wait_send()
     for s in range(2):
         sib_copy(s, 0, 0).wait_send()
-    for d in range(2):
+    for j in range(2):
         for k in range(STEPS - SUM_SLOTS, STEPS):
-            for half in range(2):
-                sum_copy(d, k, half).wait_send()
+            for part in ((0, 1) if k < STEPS - 1 else (0, 2, 3)):
+                sum_copy(j, k, part).wait_send()
+
 
 def store_kernel(h_ref, n_ref, h_hbm, n_hbm, sem):
     copies = []
@@ -269,7 +284,7 @@
                 pltpu.VMEM((BLOCK, D), jnp.bfloat16),
                 jax.ShapeDtypeStruct((2, STEPS, 2, HALF, D), jnp.float32),
             ),
-            in_specs=[hbm] * 5 + [vmem],
+            in_specs=[hbm] * 6,
             out_specs=(vmem, vmem, hbm),
             scratch_shapes=[
                 pltpu.VMEM((2, ROWS, D), jnp.bfloat16),
@@ -285,6 +300,7 @@
                 pltpu.VMEM((2, HALF, D), jnp.float32),
                 pltpu.VMEM((2, HALF, D), jnp.float32),
                 pltpu.VMEM((ROWS, D), jnp.bfloat16),
+                pltpu.VMEM((1, D), jnp.float32),
                 pltpu.SemaphoreType.DMA((2,)),
                 pltpu.SemaphoreType.DMA((3, CHUNKS)),
                 pltpu.SemaphoreType.DMA((2,)),
@@ -292,9 +308,10 @@
                 pltpu.SemaphoreType.DMA((2, STEPS)),
                 pltpu.SemaphoreType.DMA((2,)),
                 pltpu.SemaphoreType.DMA((3, STEPS)),
-                pltpu.SemaphoreType.DMA((2, SUM_SLOTS, 2)),
-                pltpu.SemaphoreType.DMA((2, STEPS, 2)),
+                pltpu.SemaphoreType.DMA((2, SUM_SLOTS, 4)),
+                pltpu.SemaphoreType.DMA((2, STEPS, 4)),
                 pltpu.SemaphoreType.DMA((2,)),
+                pltpu.SemaphoreType.DMA,
                 pltpu.SemaphoreType.DMA,
             ],
             compiler_params=pltpu.CompilerParams(collective_id=0, has_side_effects=True, vmem_limit_bytes=58000000),

time: 282 us -> 279 us (0.989)
  Pallas kernels: 281 us -> 278 us
where the time goes in v6:
time: 279 us
  Pallas kernels  278 us (100%)
    pallas_call x1, Pallas kernels, local_block(): pl.pallas_call(kernel, out_shape=(pltpu.VMEM((BLOCK, D), jnp.bfloat16), p...  275 us

profile of v6, /device:TPU:1, one launch (start us, length us, event | category | flops | bytes accessed | tf_op | source)
XLA Modules:
  0.0 278.7 jit_solution(17598424686605307342)
XLA Ops:
  0.6 274.7 %mlp_reduce.1 = (bf16[1024,2048]{1,0:T(8,128)(2,1)S(1)}, bf16[1024,2048]{1,0:T(8,128)(2,1)S(1)}, f32[2,4,2,128,2048]{4,3,2,1,0:T(8,128)}) custom-call(bf16[8192,2048]{1,0:T(8,128)(2,1)} %x_hbm.1, bf16[2048,1024]{1,0:T(8,128)(2,1)} %wg_hbm.1, bf16[2048,1024]{1,0:T(8,128)(2,1)} %wu_hbm.1, bf16[1024,2048]{1,0:T(8,128)(2,1)} %wd_hbm.1, ...), custom_call_target="tpu_custom_call" | custom-call | tf_op jit(solution)/shard_map/mlp_reduce/pallas_call | solution.py:280
  275.4 3.4 %store.1 = (bf16[1024,2048]{1,0:T(8,128)(2,1)}, bf16[1024,2048]{1,0:T(8,128)(2,1)}) custom-call(bf16[1024,2048]{1,0:T(8,128)(2,1)S(1)} %get-tuple-element.4.h_ref, bf16[1024,2048]{1,0:T(8,128)(2,1)S(1)} %get-tuple-element.5.n_ref), custom_call_target="tpu_custom_call" | custom-call | tf_op jit(solution)/shard_map/store/pallas_call | solution.py:320

commit v7 on v6

--- a/solution.py
+++ b/solution.py
@@ -10,14 +10,15 @@
 EPS = 1e-5
 ROWS = 256
 CHUNKS = 4
-COLS = (256, 256, 512)
 HALF = 128
 LATE = 32
 BLOCK = 1024
 STEPS = BLOCK // ROWS
 D = 2048
 F = 1024
-HID_SLOTS = 6
+HID_COLS = F // CHUNKS
+OUT_COLS = D // CHUNKS
+HID_SLOTS = 8
 SUM_SLOTS = 2
 FIRST = 2 * STEPS
 SECOND = FIRST + STEPS
@@ -25,8 +26,8 @@
 TILES = 8 * STEPS
 
 
-def kernel(x_hbm, wg_hbm, wu_hbm, wd_hbm, res_hbm, gain_hbm, h_ref, n_ref, sum_in, x_buf, wg, wu, wd, wd_relay, hid, tiles, hid_in, sib_in, sum_out, sum_last, sum_ld, res_ld, gain_ref,
-           x_sem, w_sem, wr_sem, relay_ssem, relay_rsem, sib_ssem, sib_rsem, sum_ssem, sum_rsem, ld_sem, res_sem, gain_sem):
+def kernel(x_hbm, wg_hbm, wu_hbm, wd_hbm, res_hbm, gain_hbm, h_ref, n_ref, sum_in, sib_own, x_buf, wg, wu, wd, wd_relay, hid, tiles, hid_in, sib_in, sum_out, sum_last, sum_ld, res_ld, sib_ld, gain_ref,
+           x_sem, w_sem, wr_sem, relay_ssem, relay_rsem, sib_ssem, sib_rsem, sum_ssem, sum_rsem, ld_sem, res_sem, sibld_sem, gain_sem):
     me = lax.axis_index("tp")
     c, cx, cy = me % 2, (me // 2) % 2, me // 4
     sib = cy * 4 + cx * 2 + (1 - c)
@@ -54,26 +55,23 @@
     def x_copy(i):
         return pltpu.make_async_copy(x_hbm.at[pl.ds(row_of(i), ROWS)], x_buf.at[i % 2], x_sem.at[i % 2])
 
-    def w_copy(j, n):
-        src, dst = ((wg_hbm, wg), (wu_hbm, wu), (wd_hbm, wd))[j]
-        cols = pl.ds(n * COLS[j], COLS[j])
-        return pltpu.make_async_copy(src.at[:, cols], dst.at[:, cols], w_sem.at[j, n])
-
+    def wd_copy(n):
+        rows = pl.ds(n * (F // CHUNKS), F // CHUNKS)
+        return pltpu.make_async_copy(wd_hbm.at[rows], wd.at[rows], w_sem.at[2 + n])
+
+    for n in range(CHUNKS):
+        wd_copy(n).start()
+    early = [pltpu.make_async_copy(wg_hbm, wg, w_sem.at[0]), pltpu.make_async_copy(wu_hbm, wu, w_sem.at[1]), pltpu.make_async_copy(gain_hbm, gain_ref, gain_sem)]
+    for copy in early:
+        copy.start()
     x_copy(0).start()
-    for n in range(CHUNKS):
-        w_copy(0, n).start()
-        w_copy(1, n).start()
-    for n in range(CHUNKS):
-        w_copy(2, n).start()
-    x_copy(1).start()
-    gain_copy = pltpu.make_async_copy(gain_hbm, gain_ref, gain_sem)
-    gain_copy.start()
 
     out_chip = (1 - c) * xn + c * yn
 
-    def w_relay_copy():
-        return pltpu.make_async_remote_copy(
-            src_ref=wd_hbm, dst_ref=wd_relay, send_sem=wr_sem.at[0], recv_sem=wr_sem.at[1],
+    def w_relay_copy(n):
+        rows = pl.ds(n * (F // CHUNKS), F // CHUNKS)
+        return pltpu.make_async_remote_copy(
+            src_ref=wd.at[rows], dst_ref=wd_relay.at[rows], send_sem=wr_sem.at[0, n], recv_sem=wr_sem.at[1, n],
             device_id={"tp": out_chip + 1 - c}, device_id_type=pl.DeviceIdType.MESH)
 
     def relay_copy(i):
@@ -82,8 +80,9 @@
             recv_sem=relay_rsem.at[i % 2, i // 2], device_id={"tp": out_chip + 1 - c}, device_id_type=pl.DeviceIdType.MESH)
 
     def sib_copy(slot, group, k):
-        return pltpu.make_async_remote_copy(
-            src_ref=tiles.at[slot], dst_ref=sib_in.at[group, k], send_sem=sib_ssem.at[slot],
+        to_hbm = isinstance(group, int) and group == 2
+        return pltpu.make_async_remote_copy(
+            src_ref=tiles.at[slot], dst_ref=sib_own.at[k] if to_hbm else sib_in.at[group, k], send_sem=sib_ssem.at[slot],
             recv_sem=sib_rsem.at[group, k], device_id={"tp": sib}, device_id_type=pl.DeviceIdType.MESH)
 
     def piece(part):
@@ -106,26 +105,15 @@
             src_ref=landing(d, k, part), dst_ref=landing(d, k, part), send_sem=sum_ssem.at[0, 0, 0], recv_sem=sum_rsem.at[d, k, part],
             device_id={"tp": sib}, device_id_type=pl.DeviceIdType.MESH)
 
-    def gate_up(x_ref, out_ref, loading=False):
-        for n in range(CHUNKS):
-            cols = slice(n * COLS[0], (n + 1) * COLS[0])
-            if loading:
-                w_copy(0, n).wait()
-                w_copy(1, n).wait()
-            gate = jnp.dot(x_ref[...], wg[:, cols], preferred_element_type=jnp.float32)
-            up = jnp.dot(x_ref[...], wu[:, cols], preferred_element_type=jnp.float32)
-            out_ref[:, cols] = (gate * jax.nn.sigmoid(gate) * up).astype(jnp.bfloat16)
-
     pl.semaphore_wait(barrier, 3)
-    w_relay_copy().start()
-    x_copy(0).wait()
-    gate_up(x_buf.at[0], hid.at[0], loading=True)
-    relay_copy(0).start()
     for n in range(CHUNKS):
-        w_copy(2, n).wait()
-    gain_copy.wait()
-
-    @pl.loop(1, TILES)
+        wd_copy(n).wait()
+        w_relay_copy(n).start()
+    w_relay_copy(0).wait_recv()
+    for copy in early:
+        copy.wait()
+
+    @pl.loop(0, TILES)
     def _(i):
         diag, to_sib, to_chip, kept = kinds(i)
         j = i % 2
@@ -153,12 +141,36 @@
         def _():
             sib_copy(j, 0, 0).wait_send()
 
+        def res_copy():
+            return pltpu.make_async_copy(res_hbm.at[pl.ds(pl.multiple_of(k_own * ROWS, ROWS), ROWS)], res_ld, res_sem)
+
+        def sib_load():
+            return pltpu.make_async_copy(sib_own.at[k_own], sib_ld, sibld_sem)
+
+        def sum_load(d, half):
+            return pltpu.make_async_copy(sum_in.at[d, k_own, half], sum_ld.at[d, pl.ds(half * HALF, HALF)], ld_sem.at[d, half])
+
         @pl.when(is_final)
         def _():
-            pltpu.make_async_copy(res_hbm.at[pl.ds(pl.multiple_of(k_own * ROWS, ROWS), ROWS)], res_ld, res_sem).start()
+            res_copy().start()
+            sib_copy(0, 2, k_own).wait_recv()
+            sib_load().start()
+            for d in range(2):
+                sum_arrival(d, k_own, 0).wait_recv()
+                sum_load(d, 0).start()
+
+            @pl.when(k_own < STEPS - 1)
+            def _():
+                for d in range(2):
+                    sum_arrival(d, k_own, 1).wait_recv()
+                    sum_load(d, 1).start()
 
         hid_slot = diag * (i % HID_SLOTS) + (1 - diag) * HID_SLOTS
-        gate_up(x_buf.at[i % 2], hid.at[hid_slot])
+        for n in range(CHUNKS):
+            cols = slice(n * HID_COLS, (n + 1) * HID_COLS)
+            gate = jnp.dot(x_buf[j], wg[:, cols], preferred_element_type=jnp.float32)
+            up = jnp.dot(x_buf[j], wu[:, cols], preferred_element_type=jnp.float32)
+            hid[hid_slot, :, cols] = (gate * jax.nn.sigmoid(gate) * up).astype(jnp.bfloat16)
 
         @pl.when(is_relay)
         def _():
@@ -168,7 +180,7 @@
         def _():
             slot = stays * 2 + (1 - stays) * j
             for n in range(CHUNKS):
-                cols = slice(n * COLS[2], (n + 1) * COLS[2])
+                cols = slice(n * OUT_COLS, (n + 1) * OUT_COLS)
                 tiles[slot, :, cols] = jnp.dot(hid[HID_SLOTS], wd[:, cols], preferred_element_type=jnp.float32).astype(jnp.bfloat16)
 
         @pl.when(is_sib)
@@ -186,7 +198,8 @@
 
             @pl.when(i == SECOND + 2)
             def _():
-                w_relay_copy().wait_recv()
+                for n in range(1, CHUNKS):
+                    w_relay_copy(n).wait_recv()
 
             @pl.when(k_chip >= SUM_SLOTS)
             def _():
@@ -194,7 +207,7 @@
                     sum_copy(j, k_chip - SUM_SLOTS, half).wait_send()
 
             for n in range(CHUNKS):
-                cols = slice(n * COLS[2], (n + 1) * COLS[2])
+                cols = slice(n * OUT_COLS, (n + 1) * OUT_COLS)
                 relayed = jnp.dot(hid_in[j, k_chip], wd_relay[:, cols], preferred_element_type=jnp.float32).astype(jnp.bfloat16)
                 total = tiles[2, :, cols].astype(jnp.float32) + sib_in[j, k_chip, :, cols].astype(jnp.float32)
                 sum_out[j, k_chip % SUM_SLOTS, :, cols] = total + relayed.astype(jnp.float32)
@@ -212,35 +225,31 @@
 
         @pl.when(is_final)
         def _():
-            sib_copy(0, 2, k_own).wait_recv()
-            pltpu.make_async_copy(res_hbm.at[pl.ds(0, ROWS)], res_ld, res_sem).wait()
+            res_copy().wait()
+            sib_load().wait()
+
             def finish(start, rows, sums, sums_start):
                 @pl.loop(0, rows // 16)
                 def _(b):
                     here = pl.ds(pl.multiple_of(sums_start + b * 16, 16), 16)
                     tile = pl.ds(pl.multiple_of(start + b * 16, 16), 16)
                     out = pl.ds(pl.multiple_of(k_own * ROWS + start + b * 16, 16), 16)
-                    y_sum = tiles[2, tile].astype(jnp.float32) + sib_in[2, k_own, tile].astype(jnp.float32)
+                    y_sum = tiles[2, tile].astype(jnp.float32) + sib_ld[tile].astype(jnp.float32)
                     y_sum = y_sum + (sums[0, here] + sums[1, here])
                     h = res_ld[tile].astype(jnp.float32) + y_sum
                     mean_sq = jnp.mean(h * h, axis=-1, keepdims=True)
                     h_ref[out] = h.astype(jnp.bfloat16)
                     n_ref[out] = (h * lax.rsqrt(mean_sq + EPS) * gain_ref[...]).astype(jnp.bfloat16)
 
-            def finish_hbm(half):
-                loads = [pltpu.make_async_copy(sum_in.at[d, k_own, half], sum_ld.at[d], ld_sem.at[d]) for d in range(2)]
+            for d in range(2):
+                sum_load(d, 0).wait()
+            finish(0, HALF, sum_ld, 0)
+
+            @pl.when(k_own < STEPS - 1)
+            def _():
                 for d in range(2):
-                    sum_arrival(d, k_own, half).wait_recv()
-                    loads[d].start()
-                for load in loads:
-                    load.wait()
-                finish(half * HALF, HALF, sum_ld, 0)
-
-            finish_hbm(0)
-
-            @pl.when(k_own < STEPS - 1)
-            def _():
-                finish_hbm(1)
+                    sum_load(d, 1).wait()
+                finish(HALF, HALF, sum_ld, HALF)
 
             @pl.when(k_own == STEPS - 1)
             def _():
@@ -250,7 +259,8 @@
                     start = (part - 2) * (HALF - LATE)
                     finish(HALF + start, rows, sum_last, start)
 
-    w_relay_copy().wait_send()
+    for n in range(CHUNKS):
+        w_relay_copy(n).wait_send()
     for s in range(HID_SLOTS):
         relay_copy(FIRST - HID_SLOTS + s).wait_send()
     for s in range(2):
@@ -277,15 +287,16 @@
     def local_block(x_in, w_gate, w_up, w_down, residual, norm_gain):
         hbm = pl.BlockSpec(memory_space=pltpu.HBM)
         vmem = pl.BlockSpec(memory_space=pltpu.VMEM)
-        h, n, _ = pl.pallas_call(
+        h, n, _, _ = pl.pallas_call(
             kernel,
             out_shape=(
                 pltpu.VMEM((BLOCK, D), jnp.bfloat16),
                 pltpu.VMEM((BLOCK, D), jnp.bfloat16),
                 jax.ShapeDtypeStruct((2, STEPS, 2, HALF, D), jnp.float32),
+                jax.ShapeDtypeStruct((STEPS, ROWS, D), jnp.bfloat16),
             ),
             in_specs=[hbm] * 6,
-            out_specs=(vmem, vmem, hbm),
+            out_specs=(vmem, vmem, hbm, hbm),
             scratch_shapes=[
                 pltpu.VMEM((2, ROWS, D), jnp.bfloat16),
                 pltpu.VMEM((D, F), jnp.bfloat16),
@@ -295,22 +306,24 @@
                 pltpu.VMEM((HID_SLOTS + 1, ROWS, F), jnp.bfloat16),
                 pltpu.VMEM((3, ROWS, D), jnp.bfloat16),
                 pltpu.VMEM((2, STEPS, ROWS, F), jnp.bfloat16),
-                pltpu.VMEM((3, STEPS, ROWS, D), jnp.bfloat16),
+                pltpu.VMEM((2, STEPS, ROWS, D), jnp.bfloat16),
                 pltpu.VMEM((2, SUM_SLOTS, ROWS, D), jnp.float32),
                 pltpu.VMEM((2, HALF, D), jnp.float32),
-                pltpu.VMEM((2, HALF, D), jnp.float32),
+                pltpu.VMEM((2, ROWS, D), jnp.float32),
+                pltpu.VMEM((ROWS, D), jnp.bfloat16),
                 pltpu.VMEM((ROWS, D), jnp.bfloat16),
                 pltpu.VMEM((1, D), jnp.float32),
                 pltpu.SemaphoreType.DMA((2,)),
-                pltpu.SemaphoreType.DMA((3, CHUNKS)),
-                pltpu.SemaphoreType.DMA((2,)),
+                pltpu.SemaphoreType.DMA((2 + CHUNKS,)),
+                pltpu.SemaphoreType.DMA((2, CHUNKS)),
                 pltpu.SemaphoreType.DMA((HID_SLOTS,)),
                 pltpu.SemaphoreType.DMA((2, STEPS)),
                 pltpu.SemaphoreType.DMA((2,)),
                 pltpu.SemaphoreType.DMA((3, STEPS)),
                 pltpu.SemaphoreType.DMA((2, SUM_SLOTS, 4)),
                 pltpu.SemaphoreType.DMA((2, STEPS, 4)),
-                pltpu.SemaphoreType.DMA((2,)),
+                pltpu.SemaphoreType.DMA((2, 2)),
+                pltpu.SemaphoreType.DMA,
                 pltpu.SemaphoreType.DMA,
                 pltpu.SemaphoreType.DMA,
             ],

time: 279 us -> 280 us (level)
  no operation moved by 1% of the time
where the time goes in v7:
time: 280 us
  Pallas kernels  279 us (100%)
    pallas_call x1, Pallas kernels, local_block(): pl.pallas_call(kernel, out_shape=(pltpu.VMEM((BLOCK, D), jnp.bfloat16), p...  276 us

profile of v7, /device:TPU:1, one launch (start us, length us, event | category | flops | bytes accessed | tf_op | source)
XLA Modules:
  0.0 280.0 jit_solution(7905624890403897017)
XLA Ops:
  0.6 276.0 %mlp_reduce.1 = (bf16[1024,2048]{1,0:T(8,128)(2,1)S(1)}, bf16[1024,2048]{1,0:T(8,128)(2,1)S(1)}, f32[2,4,2,128,2048]{4,3,2,1,0:T(8,128)}, bf16[4,256,2048]{2,1,0:T(8,128)(2,1)}) custom-call(bf16[8192,2048]{1,0:T(8,128)(2,1)} %x_hbm.1, bf16[2048,1024]{1,0:T(8,128)(2,1)} %wg_hbm.1, bf16[2048,1024]{1,0:T(8,128)(2,1)} %wu_hbm.1, bf16[1024,2048]{1,0:T(8,128)(2,1)} %wd_hbm.1, ...), custom_call_target="tpu_custom_call" | custom-call | tf_op jit(solution)/shard_map/mlp_reduce/pallas_call | solution.py:290
  276.6 3.4 %store.1 = (bf16[1024,2048]{1,0:T(8,128)(2,1)}, bf16[1024,2048]{1,0:T(8,128)(2,1)}) custom-call(bf16[1024,2048]{1,0:T(8,128)(2,1)S(1)} %get-tuple-element.4.h_ref, bf16[1024,2048]{1,0:T(8,128)(2,1)S(1)} %get-tuple-element.5.n_ref), custom_call_target="tpu_custom_call" | custom-call | tf_op jit(solution)/shard_map/store/pallas_call | solution.py:333

commit v8 on v7

--- a/solution.py
+++ b/solution.py
@@ -27,7 +27,7 @@
 
 
 def kernel(x_hbm, wg_hbm, wu_hbm, wd_hbm, res_hbm, gain_hbm, h_ref, n_ref, sum_in, sib_own, x_buf, wg, wu, wd, wd_relay, hid, tiles, hid_in, sib_in, sum_out, sum_last, sum_ld, res_ld, sib_ld, gain_ref,
-           x_sem, w_sem, wr_sem, relay_ssem, relay_rsem, sib_ssem, sib_rsem, sum_ssem, sum_rsem, ld_sem, res_sem, sibld_sem, gain_sem):
+           x_sem, w_sem, wr_sem, relay_ssem, relay_rsem, sib_ssem, sib_rsem, sum_ssem, sum_rsem, ld_sem, res_sem, sibld_sem):
     me = lax.axis_index("tp")
     c, cx, cy = me % 2, (me // 2) % 2, me // 4
     sib = cy * 4 + cx * 2 + (1 - c)
@@ -55,13 +55,7 @@
     def x_copy(i):
         return pltpu.make_async_copy(x_hbm.at[pl.ds(row_of(i), ROWS)], x_buf.at[i % 2], x_sem.at[i % 2])
 
-    def wd_copy(n):
-        rows = pl.ds(n * (F // CHUNKS), F // CHUNKS)
-        return pltpu.make_async_copy(wd_hbm.at[rows], wd.at[rows], w_sem.at[2 + n])
-
-    for n in range(CHUNKS):
-        wd_copy(n).start()
-    early = [pltpu.make_async_copy(wg_hbm, wg, w_sem.at[0]), pltpu.make_async_copy(wu_hbm, wu, w_sem.at[1]), pltpu.make_async_copy(gain_hbm, gain_ref, gain_sem)]
+    early = [pltpu.make_async_copy(src, dst, w_sem.at[n]) for n, (src, dst) in enumerate(((wg_hbm, wg), (wu_hbm, wu), (wd_hbm, wd), (gain_hbm, gain_ref)))]
     for copy in early:
         copy.start()
     x_copy(0).start()
@@ -69,9 +63,9 @@
     out_chip = (1 - c) * xn + c * yn
 
     def w_relay_copy(n):
-        rows = pl.ds(n * (F // CHUNKS), F // CHUNKS)
-        return pltpu.make_async_remote_copy(
-            src_ref=wd.at[rows], dst_ref=wd_relay.at[rows], send_sem=wr_sem.at[0, n], recv_sem=wr_sem.at[1, n],
+        rows = (pl.ds(0, 128), pl.ds(128, F - 128))[n]
+        return pltpu.make_async_remote_copy(
+            src_ref=wd_hbm.at[rows], dst_ref=wd_relay.at[rows], send_sem=wr_sem.at[0, n], recv_sem=wr_sem.at[1, n],
             device_id={"tp": out_chip + 1 - c}, device_id_type=pl.DeviceIdType.MESH)
 
     def relay_copy(i):
@@ -106,8 +100,7 @@
             device_id={"tp": sib}, device_id_type=pl.DeviceIdType.MESH)
 
     pl.semaphore_wait(barrier, 3)
-    for n in range(CHUNKS):
-        wd_copy(n).wait()
+    for n in range(2):
         w_relay_copy(n).start()
     w_relay_copy(0).wait_recv()
     for copy in early:
@@ -198,8 +191,7 @@
 
             @pl.when(i == SECOND + 2)
             def _():
-                for n in range(1, CHUNKS):
-                    w_relay_copy(n).wait_recv()
+                w_relay_copy(1).wait_recv()
 
             @pl.when(k_chip >= SUM_SLOTS)
             def _():
@@ -259,7 +251,7 @@
                     start = (part - 2) * (HALF - LATE)
                     finish(HALF + start, rows, sum_last, start)
 
-    for n in range(CHUNKS):
+    for n in range(2):
         w_relay_copy(n).wait_send()
     for s in range(HID_SLOTS):
         relay_copy(FIRST - HID_SLOTS + s).wait_send()
@@ -314,8 +306,8 @@
                 pltpu.VMEM((ROWS, D), jnp.bfloat16),
                 pltpu.VMEM((1, D), jnp.float32),
                 pltpu.SemaphoreType.DMA((2,)),
-                pltpu.SemaphoreType.DMA((2 + CHUNKS,)),
-                pltpu.SemaphoreType.DMA((2, CHUNKS)),
+                pltpu.SemaphoreType.DMA((4,)),
+                pltpu.SemaphoreType.DMA((2, 2)),
                 pltpu.SemaphoreType.DMA((HID_SLOTS,)),
                 pltpu.SemaphoreType.DMA((2, STEPS)),
                 pltpu.SemaphoreType.DMA((2,)),
@@ -323,7 +315,6 @@
                 pltpu.SemaphoreType.DMA((2, SUM_SLOTS, 4)),
                 pltpu.SemaphoreType.DMA((2, STEPS, 4)),
                 pltpu.SemaphoreType.DMA((2, 2)),
-                pltpu.SemaphoreType.DMA,
                 pltpu.SemaphoreType.DMA,
                 pltpu.SemaphoreType.DMA,
             ],

time: 280 us -> 279 us (level)
  no operation moved by 1% of the time
where the time goes in v8:
time: 279 us
  Pallas kernels  278 us (100%)
    pallas_call x1, Pallas kernels, local_block(): pl.pallas_call(kernel, out_shape=(pltpu.VMEM((BLOCK, D), jnp.bfloat16), p...  275 us

profile of v8, /device:TPU:1, one launch (start us, length us, event | category | flops | bytes accessed | tf_op | source)
XLA Modules:
  0.0 278.7 jit_solution(1680803718586674936)
XLA Ops:
  0.6 274.7 %mlp_reduce.1 = (bf16[1024,2048]{1,0:T(8,128)(2,1)S(1)}, bf16[1024,2048]{1,0:T(8,128)(2,1)S(1)}, f32[2,4,2,128,2048]{4,3,2,1,0:T(8,128)}, bf16[4,256,2048]{2,1,0:T(8,128)(2,1)}) custom-call(bf16[8192,2048]{1,0:T(8,128)(2,1)} %x_hbm.1, bf16[2048,1024]{1,0:T(8,128)(2,1)} %wg_hbm.1, bf16[2048,1024]{1,0:T(8,128)(2,1)} %wu_hbm.1, bf16[1024,2048]{1,0:T(8,128)(2,1)} %wd_hbm.1, ...), custom_call_target="tpu_custom_call" | custom-call | tf_op jit(solution)/shard_map/mlp_reduce/pallas_call | solution.py:282
  275.3 3.4 %store.1 = (bf16[1024,2048]{1,0:T(8,128)(2,1)}, bf16[1024,2048]{1,0:T(8,128)(2,1)}) custom-call(bf16[1024,2048]{1,0:T(8,128)(2,1)S(1)} %get-tuple-element.4.h_ref, bf16[1024,2048]{1,0:T(8,128)(2,1)S(1)} %get-tuple-element.5.n_ref), custom_call_target="tpu_custom_call" | custom-call | tf_op jit(solution)/shard_map/store/pallas_call | solution.py:324

commit v9 on v8

--- a/solution.py
+++ b/solution.py
@@ -11,14 +11,13 @@
 ROWS = 256
 CHUNKS = 4
 HALF = 128
-LATE = 32
+LATE = 16
 BLOCK = 1024
 STEPS = BLOCK // ROWS
 D = 2048
 F = 1024
 HID_COLS = F // CHUNKS
 OUT_COLS = D // CHUNKS
-HID_SLOTS = 8
 SUM_SLOTS = 2
 FIRST = 2 * STEPS
 SECOND = FIRST + STEPS
@@ -27,7 +26,7 @@
 
 
 def kernel(x_hbm, wg_hbm, wu_hbm, wd_hbm, res_hbm, gain_hbm, h_ref, n_ref, sum_in, sib_own, x_buf, wg, wu, wd, wd_relay, hid, tiles, hid_in, sib_in, sum_out, sum_last, sum_ld, res_ld, sib_ld, gain_ref,
-           x_sem, w_sem, wr_sem, relay_ssem, relay_rsem, sib_ssem, sib_rsem, sum_ssem, sum_rsem, ld_sem, res_sem, sibld_sem):
+           x_sem, w_sem, wr_sem, relay_ssem, relay_rsem, sib_ssem, sib_rsem, sum_ssem, sum_rsem, ld_sem, res_sem, sibld_sem, ready):
     me = lax.axis_index("tp")
     c, cx, cy = me % 2, (me // 2) % 2, me // 4
     sib = cy * 4 + cx * 2 + (1 - c)
@@ -35,7 +34,8 @@
     yn = (1 - cy) * 4 + cx * 2
 
     barrier = pltpu.get_barrier_semaphore()
-    for dev in (sib, (1 - c) * (yn + 1) + c * xn, (1 - c) * xn + c * (yn + 1)):
+    source = (1 - c) * (yn + 1) + c * xn
+    for dev in (sib, source):
         pl.semaphore_signal(barrier, inc=1, device_id={"tp": dev}, device_id_type=pl.DeviceIdType.MESH)
 
     def kinds(i):
@@ -70,7 +70,7 @@
 
     def relay_copy(i):
         return pltpu.make_async_remote_copy(
-            src_ref=hid.at[i % HID_SLOTS], dst_ref=hid_in.at[i % 2, i // 2], send_sem=relay_ssem.at[i % HID_SLOTS],
+            src_ref=hid.at[i], dst_ref=hid_in.at[i % 2, i // 2], send_sem=relay_ssem,
             recv_sem=relay_rsem.at[i % 2, i // 2], device_id={"tp": out_chip + 1 - c}, device_id_type=pl.DeviceIdType.MESH)
 
     def sib_copy(slot, group, k):
@@ -79,30 +79,32 @@
             src_ref=tiles.at[slot], dst_ref=sib_own.at[k] if to_hbm else sib_in.at[group, k], send_sem=sib_ssem.at[slot],
             recv_sem=sib_rsem.at[group, k], device_id={"tp": sib}, device_id_type=pl.DeviceIdType.MESH)
 
-    def piece(part):
-        return (pl.ds(0, HALF), pl.ds(HALF, HALF), pl.ds(HALF, HALF - LATE), pl.ds(ROWS - LATE, LATE))[part]
+    last = STEPS - 1
+    parts = ((0, HALF), (HALF, HALF - LATE), (ROWS - LATE, LATE))
 
     def landing(d, k, part):
-        if part < 2:
-            return sum_in.at[d, k, part]
-        return sum_last.at[d, pl.ds(0, HALF - LATE) if part == 2 else pl.ds(HALF - LATE, LATE)]
-
-    def sum_copy(j, k, part):
+        if part is None:
+            return sum_in.at[d, k]
+        start, rows = parts[part]
+        return sum_in.at[d, last, pl.ds(0, HALF)] if part == 0 else sum_last.at[d, pl.ds(start - HALF, rows)]
+
+    def sum_copy(j, k, part=None):
         slot = k % SUM_SLOTS
         return pltpu.make_async_remote_copy(
-            src_ref=sum_out.at[j, slot, piece(part)], dst_ref=landing(c, k, part),
-            send_sem=sum_ssem.at[j, slot, part], recv_sem=sum_rsem.at[c, k, part],
+            src_ref=sum_out.at[j, slot] if part is None else sum_out.at[j, slot, pl.ds(*parts[part])], dst_ref=landing(c, k, part),
+            send_sem=sum_ssem.at[j, slot + (part or 0)], recv_sem=sum_rsem.at[c, k + (part or 0)],
             device_id={"tp": out_chip + j}, device_id_type=pl.DeviceIdType.MESH)
 
-    def sum_arrival(d, k, part):
-        return pltpu.make_async_remote_copy(
-            src_ref=landing(d, k, part), dst_ref=landing(d, k, part), send_sem=sum_ssem.at[0, 0, 0], recv_sem=sum_rsem.at[d, k, part],
+    def sum_arrival(d, k, part=None):
+        return pltpu.make_async_remote_copy(
+            src_ref=landing(d, k, part), dst_ref=landing(d, k, part), send_sem=sum_ssem.at[0, 0], recv_sem=sum_rsem.at[d, k + (part or 0)],
             device_id={"tp": sib}, device_id_type=pl.DeviceIdType.MESH)
 
-    pl.semaphore_wait(barrier, 3)
+    pl.semaphore_wait(barrier, 2)
     for n in range(2):
         w_relay_copy(n).start()
     w_relay_copy(0).wait_recv()
+    pl.semaphore_signal(ready, inc=1, device_id={"tp": source}, device_id_type=pl.DeviceIdType.MESH)
     for copy in early:
         copy.wait()
 
@@ -126,10 +128,6 @@
 
         x_copy(i).wait()
 
-        @pl.when(jnp.logical_and(is_relay, i >= HID_SLOTS))
-        def _():
-            relay_copy(i - HID_SLOTS).wait_send()
-
         @pl.when(jnp.logical_and(jnp.logical_or(is_sib, is_own_sib), i >= FIRST + 2))
         def _():
             sib_copy(j, 0, 0).wait_send()
@@ -140,25 +138,28 @@
         def sib_load():
             return pltpu.make_async_copy(sib_own.at[k_own], sib_ld, sibld_sem)
 
-        def sum_load(d, half):
-            return pltpu.make_async_copy(sum_in.at[d, k_own, half], sum_ld.at[d, pl.ds(half * HALF, HALF)], ld_sem.at[d, half])
+        def sum_load(d, rows):
+            return pltpu.make_async_copy(sum_in.at[d, k_own, pl.ds(0, rows)], sum_ld.at[d, pl.ds(0, rows)], ld_sem.at[d])
 
         @pl.when(is_final)
         def _():
             res_copy().start()
             sib_copy(0, 2, k_own).wait_recv()
             sib_load().start()
-            for d in range(2):
-                sum_arrival(d, k_own, 0).wait_recv()
-                sum_load(d, 0).start()
-
-            @pl.when(k_own < STEPS - 1)
+
+            @pl.when(k_own < last)
             def _():
                 for d in range(2):
-                    sum_arrival(d, k_own, 1).wait_recv()
-                    sum_load(d, 1).start()
-
-        hid_slot = diag * (i % HID_SLOTS) + (1 - diag) * HID_SLOTS
+                    sum_arrival(d, k_own).wait_recv()
+                    sum_load(d, ROWS).start()
+
+            @pl.when(k_own == last)
+            def _():
+                for d in range(2):
+                    sum_arrival(d, last, 0).wait_recv()
+                    sum_load(d, HALF).start()
+
+        hid_slot = diag * i + (1 - diag) * FIRST
         for n in range(CHUNKS):
             cols = slice(n * HID_COLS, (n + 1) * HID_COLS)
             gate = jnp.dot(x_buf[j], wg[:, cols], preferred_element_type=jnp.float32)
@@ -174,7 +175,7 @@
             slot = stays * 2 + (1 - stays) * j
             for n in range(CHUNKS):
                 cols = slice(n * OUT_COLS, (n + 1) * OUT_COLS)
-                tiles[slot, :, cols] = jnp.dot(hid[HID_SLOTS], wd[:, cols], preferred_element_type=jnp.float32).astype(jnp.bfloat16)
+                tiles[slot, :, cols] = jnp.dot(hid[FIRST], wd[:, cols], preferred_element_type=jnp.float32).astype(jnp.bfloat16)
 
         @pl.when(is_sib)
         def _():
@@ -192,11 +193,11 @@
             @pl.when(i == SECOND + 2)
             def _():
                 w_relay_copy(1).wait_recv()
+                pl.semaphore_wait(ready, 1)
 
             @pl.when(k_chip >= SUM_SLOTS)
             def _():
-                for half in range(2):
-                    sum_copy(j, k_chip - SUM_SLOTS, half).wait_send()
+                sum_copy(j, k_chip - SUM_SLOTS).wait_send()
 
             for n in range(CHUNKS):
                 cols = slice(n * OUT_COLS, (n + 1) * OUT_COLS)
@@ -204,16 +205,14 @@
                 total = tiles[2, :, cols].astype(jnp.float32) + sib_in[j, k_chip, :, cols].astype(jnp.float32)
                 sum_out[j, k_chip % SUM_SLOTS, :, cols] = total + relayed.astype(jnp.float32)
 
-            sum_copy(j, k_chip, 0).start()
-
-            @pl.when(k_chip < STEPS - 1)
-            def _():
-                sum_copy(j, k_chip, 1).start()
-
-            @pl.when(k_chip == STEPS - 1)
-            def _():
-                for part in (2, 3):
-                    sum_copy(j, k_chip, part).start()
+            @pl.when(k_chip < last)
+            def _():
+                sum_copy(j, k_chip).start()
+
+            @pl.when(k_chip == last)
+            def _():
+                for part in range(3):
+                    sum_copy(j, last, part).start()
 
         @pl.when(is_final)
         def _():
@@ -233,34 +232,33 @@
                     h_ref[out] = h.astype(jnp.bfloat16)
                     n_ref[out] = (h * lax.rsqrt(mean_sq + EPS) * gain_ref[...]).astype(jnp.bfloat16)
 
-            for d in range(2):
-                sum_load(d, 0).wait()
-            finish(0, HALF, sum_ld, 0)
-
-            @pl.when(k_own < STEPS - 1)
+            @pl.when(k_own < last)
             def _():
                 for d in range(2):
-                    sum_load(d, 1).wait()
-                finish(HALF, HALF, sum_ld, HALF)
-
-            @pl.when(k_own == STEPS - 1)
-            def _():
-                for part, rows in ((2, HALF - LATE), (3, LATE)):
+                    sum_load(d, ROWS).wait()
+                finish(0, ROWS, sum_ld, 0)
+
+            @pl.when(k_own == last)
+            def _():
+                for d in range(2):
+                    sum_load(d, HALF).wait()
+                finish(0, HALF, sum_ld, 0)
+                for part in (1, 2):
                     for d in range(2):
-                        sum_arrival(d, STEPS - 1, part).wait_recv()
-                    start = (part - 2) * (HALF - LATE)
-                    finish(HALF + start, rows, sum_last, start)
+                        sum_arrival(d, last, part).wait_recv()
+                    start, rows = parts[part]
+                    finish(start, rows, sum_last, start - HALF)
 
     for n in range(2):
         w_relay_copy(n).wait_send()
-    for s in range(HID_SLOTS):
-        relay_copy(FIRST - HID_SLOTS + s).wait_send()
+    sent = hid.at[pl.ds(0, FIRST)]
+    pltpu.make_async_copy(sent, sent, relay_ssem).wait()
     for s in range(2):
         sib_copy(s, 0, 0).wait_send()
     for j in range(2):
-        for k in range(STEPS - SUM_SLOTS, STEPS):
-            for part in ((0, 1) if k < STEPS - 1 else (0, 2, 3)):
-                sum_copy(j, k, part).wait_send()
+        sum_copy(j, last - 1).wait_send()
+        for part in range(3):
+            sum_copy(j, last, part).wait_send()
 
 
 def store_kernel(h_ref, n_ref, h_hbm, n_hbm, sem):
@@ -284,7 +282,7 @@
             out_shape=(
                 pltpu.VMEM((BLOCK, D), jnp.bfloat16),
                 pltpu.VMEM((BLOCK, D), jnp.bfloat16),
-                jax.ShapeDtypeStruct((2, STEPS, 2, HALF, D), jnp.float32),
+                jax.ShapeDtypeStruct((2, STEPS, ROWS, D), jnp.float32),
                 jax.ShapeDtypeStruct((STEPS, ROWS, D), jnp.bfloat16),
             ),
             in_specs=[hbm] * 6,
@@ -295,7 +293,7 @@
                 pltpu.VMEM((D, F), jnp.bfloat16),
                 pltpu.VMEM((F, D), jnp.bfloat16),
                 pltpu.VMEM((F, D), jnp.bfloat16),
-                pltpu.VMEM((HID_SLOTS + 1, ROWS, F), jnp.bfloat16),
+                pltpu.VMEM((FIRST + 1, ROWS, F), jnp.bfloat16),
                 pltpu.VMEM((3, ROWS, D), jnp.bfloat16),
                 pltpu.VMEM((2, STEPS, ROWS, F), jnp.bfloat16),
                 pltpu.VMEM((2, STEPS, ROWS, D), jnp.bfloat16),
@@ -308,15 +306,16 @@
                 pltpu.SemaphoreType.DMA((2,)),
                 pltpu.SemaphoreType.DMA((4,)),
                 pltpu.SemaphoreType.DMA((2, 2)),
-                pltpu.SemaphoreType.DMA((HID_SLOTS,)),
+                pltpu.SemaphoreType.DMA,
                 pltpu.SemaphoreType.DMA((2, STEPS)),
                 pltpu.SemaphoreType.DMA((2,)),
                 pltpu.SemaphoreType.DMA((3, STEPS)),
-                pltpu.SemaphoreType.DMA((2, SUM_SLOTS, 4)),
-                pltpu.SemaphoreType.DMA((2, STEPS, 4)),
-                pltpu.SemaphoreType.DMA((2, 2)),
+                pltpu.SemaphoreType.DMA((2, SUM_SLOTS + 2)),
+                pltpu.SemaphoreType.DMA((2, STEPS + 2)),
+                pltpu.SemaphoreType.DMA((2,)),
                 pltpu.SemaphoreType.DMA,
                 pltpu.SemaphoreType.DMA,
+                pltpu.SemaphoreType.REGULAR,
             ],
             compiler_params=pltpu.CompilerParams(collective_id=0, has_side_effects=True, vmem_limit_bytes=58000000),
             name="mlp_reduce",

time: 279 us -> 278 us (level)
  no operation moved by 1% of the time
where the time goes in v9:
time: 278 us
  Pallas kernels  278 us (100%)
    pallas_call x1, Pallas kernels, local_block(): pl.pallas_call(kernel, out_shape=(pltpu.VMEM((BLOCK, D), jnp.bfloat16), p...  274 us

profile of v9, /device:TPU:1, one launch (start us, length us, event | category | flops | bytes accessed | tf_op | source)
XLA Modules:
  0.0 278.2 jit_solution(2620151152334198628)
XLA Ops:
  0.6 274.2 %mlp_reduce.1 = (bf16[1024,2048]{1,0:T(8,128)(2,1)S(1)}, bf16[1024,2048]{1,0:T(8,128)(2,1)S(1)}, f32[2,4,256,2048]{3,2,1,0:T(8,128)}, bf16[4,256,2048]{2,1,0:T(8,128)(2,1)}) custom-call(bf16[8192,2048]{1,0:T(8,128)(2,1)} %x_hbm.1, bf16[2048,1024]{1,0:T(8,128)(2,1)} %wg_hbm.1, bf16[2048,1024]{1,0:T(8,128)(2,1)} %wu_hbm.1, bf16[1024,2048]{1,0:T(8,128)(2,1)} %wd_hbm.1, ...), custom_call_target="tpu_custom_call" | custom-call | tf_op jit(solution)/shard_map/mlp_reduce/pallas_call | solution.py:280
  274.9 3.4 %store.1 = (bf16[1024,2048]{1,0:T(8,128)(2,1)}, bf16[1024,2048]{1,0:T(8,128)(2,1)}) custom-call(bf16[1024,2048]{1,0:T(8,128)(2,1)S(1)} %get-tuple-element.4.h_ref, bf16[1024,2048]{1,0:T(8,128)(2,1)S(1)} %get-tuple-element.5.n_ref), custom_call_target="tpu_custom_call" | custom-call | tf_op jit(solution)/shard_map/store/pallas_call | solution.py:323

commit v10 on v9

--- a/solution.py
+++ b/solution.py
@@ -19,6 +19,7 @@
 HID_COLS = F // CHUNKS
 OUT_COLS = D // CHUNKS
 SUM_SLOTS = 2
+GROUP = 4
 FIRST = 2 * STEPS
 SECOND = FIRST + STEPS
 THIRD = SECOND + 4 * STEPS
@@ -26,7 +27,7 @@
 
 
 def kernel(x_hbm, wg_hbm, wu_hbm, wd_hbm, res_hbm, gain_hbm, h_ref, n_ref, sum_in, sib_own, x_buf, wg, wu, wd, wd_relay, hid, tiles, hid_in, sib_in, sum_out, sum_last, sum_ld, res_ld, sib_ld, gain_ref,
-           x_sem, w_sem, wr_sem, relay_ssem, relay_rsem, sib_ssem, sib_rsem, sum_ssem, sum_rsem, ld_sem, res_sem, sibld_sem, ready):
+           x_sem, w_sem, wr_sem, relay_sem, sib_ssem, sib_rsem, sum_ssem, sum_rsem, ld_sem, res_sem, sibld_sem, ready):
     me = lax.axis_index("tp")
     c, cx, cy = me % 2, (me // 2) % 2, me // 4
     sib = cy * 4 + cx * 2 + (1 - c)
@@ -68,10 +69,11 @@
             src_ref=wd_hbm.at[rows], dst_ref=wd_relay.at[rows], send_sem=wr_sem.at[0, n], recv_sem=wr_sem.at[1, n],
             device_id={"tp": out_chip + 1 - c}, device_id_type=pl.DeviceIdType.MESH)
 
-    def relay_copy(i):
-        return pltpu.make_async_remote_copy(
-            src_ref=hid.at[i], dst_ref=hid_in.at[i % 2, i // 2], send_sem=relay_ssem,
-            recv_sem=relay_rsem.at[i % 2, i // 2], device_id={"tp": out_chip + 1 - c}, device_id_type=pl.DeviceIdType.MESH)
+    def relay_copy(g):
+        group = pl.ds(g * GROUP, GROUP)
+        return pltpu.make_async_remote_copy(
+            src_ref=hid.at[group], dst_ref=hid_in.at[group], send_sem=relay_sem.at[0, g], recv_sem=relay_sem.at[1, g],
+            device_id={"tp": out_chip + 1 - c}, device_id_type=pl.DeviceIdType.MESH)
 
     def sib_copy(slot, group, k):
         to_hbm = isinstance(group, int) and group == 2
@@ -141,19 +143,21 @@
         def sum_load(d, rows):
             return pltpu.make_async_copy(sum_in.at[d, k_own, pl.ds(0, rows)], sum_ld.at[d, pl.ds(0, rows)], ld_sem.at[d])
 
+        late_own = jnp.logical_and(k_own == last, c == 1)
+
         @pl.when(is_final)
         def _():
             res_copy().start()
             sib_copy(0, 2, k_own).wait_recv()
             sib_load().start()
 
-            @pl.when(k_own < last)
+            @pl.when(jnp.logical_not(late_own))
             def _():
                 for d in range(2):
                     sum_arrival(d, k_own).wait_recv()
                     sum_load(d, ROWS).start()
 
-            @pl.when(k_own == last)
+            @pl.when(late_own)
             def _():
                 for d in range(2):
                     sum_arrival(d, last, 0).wait_recv()
@@ -166,9 +170,9 @@
             up = jnp.dot(x_buf[j], wu[:, cols], preferred_element_type=jnp.float32)
             hid[hid_slot, :, cols] = (gate * jax.nn.sigmoid(gate) * up).astype(jnp.bfloat16)
 
-        @pl.when(is_relay)
-        def _():
-            relay_copy(i).start()
+        @pl.when(jnp.logical_and(is_relay, i % GROUP == GROUP - 1))
+        def _():
+            relay_copy(i // GROUP).start()
 
         @pl.when(i >= FIRST)
         def _():
@@ -188,7 +192,10 @@
         @pl.when(is_sum)
         def _():
             sib_copy(0, j, k_chip).wait_recv()
-            relay_copy(2 * k_chip + j).wait_recv()
+
+            @pl.when((2 * k_chip + j) % GROUP == 0)
+            def _():
+                relay_copy((2 * k_chip + j) // GROUP).wait_recv()
 
             @pl.when(i == SECOND + 2)
             def _():
@@ -201,18 +208,20 @@
 
             for n in range(CHUNKS):
                 cols = slice(n * OUT_COLS, (n + 1) * OUT_COLS)
-                relayed = jnp.dot(hid_in[j, k_chip], wd_relay[:, cols], preferred_element_type=jnp.float32).astype(jnp.bfloat16)
+                relayed = jnp.dot(hid_in[2 * k_chip + j], wd_relay[:, cols], preferred_element_type=jnp.float32).astype(jnp.bfloat16)
                 total = tiles[2, :, cols].astype(jnp.float32) + sib_in[j, k_chip, :, cols].astype(jnp.float32)
                 sum_out[j, k_chip % SUM_SLOTS, :, cols] = total + relayed.astype(jnp.float32)
 
-            @pl.when(k_chip < last)
+            late = jnp.logical_and(k_chip == last, j == 1)
+
+            @pl.when(jnp.logical_not(late))
             def _():
                 sum_copy(j, k_chip).start()
 
-            @pl.when(k_chip == last)
+            @pl.when(late)
             def _():
                 for part in range(3):
-                    sum_copy(j, last, part).start()
+                    sum_copy(1, last, part).start()
 
         @pl.when(is_final)
         def _():
@@ -232,13 +241,13 @@
                     h_ref[out] = h.astype(jnp.bfloat16)
                     n_ref[out] = (h * lax.rsqrt(mean_sq + EPS) * gain_ref[...]).astype(jnp.bfloat16)
 
-            @pl.when(k_own < last)
+            @pl.when(jnp.logical_not(late_own))
             def _():
                 for d in range(2):
                     sum_load(d, ROWS).wait()
                 finish(0, ROWS, sum_ld, 0)
 
-            @pl.when(k_own == last)
+            @pl.when(late_own)
             def _():
                 for d in range(2):
                     sum_load(d, HALF).wait()
@@ -251,14 +260,15 @@
 
     for n in range(2):
         w_relay_copy(n).wait_send()
-    sent = hid.at[pl.ds(0, FIRST)]
-    pltpu.make_async_copy(sent, sent, relay_ssem).wait()
+    for g in range(FIRST // GROUP):
+        relay_copy(g).wait_send()
     for s in range(2):
         sib_copy(s, 0, 0).wait_send()
     for j in range(2):
         sum_copy(j, last - 1).wait_send()
-        for part in range(3):
-            sum_copy(j, last, part).wait_send()
+    sum_copy(0, last).wait_send()
+    for part in range(3):
+        sum_copy(1, last, part).wait_send()
 
 
 def store_kernel(h_ref, n_ref, h_hbm, n_hbm, sem):
@@ -295,7 +305,7 @@
                 pltpu.VMEM((F, D), jnp.bfloat16),
                 pltpu.VMEM((FIRST + 1, ROWS, F), jnp.bfloat16),
                 pltpu.VMEM((3, ROWS, D), jnp.bfloat16),
-                pltpu.VMEM((2, STEPS, ROWS, F), jnp.bfloat16),
+                pltpu.VMEM((FIRST, ROWS, F), jnp.bfloat16),
                 pltpu.VMEM((2, STEPS, ROWS, D), jnp.bfloat16),
                 pltpu.VMEM((2, SUM_SLOTS, ROWS, D), jnp.float32),
                 pltpu.VMEM((2, HALF, D), jnp.float32),
@@ -306,8 +316,7 @@
                 pltpu.SemaphoreType.DMA((2,)),
                 pltpu.SemaphoreType.DMA((4,)),
                 pltpu.SemaphoreType.DMA((2, 2)),
-                pltpu.SemaphoreType.DMA,
-                pltpu.SemaphoreType.DMA((2, STEPS)),
+                pltpu.SemaphoreType.DMA((2, FIRST // GROUP)),
                 pltpu.SemaphoreType.DMA((2,)),
                 pltpu.SemaphoreType.DMA((3, STEPS)),
                 pltpu.SemaphoreType.DMA((2, SUM_SLOTS + 2)),

time: 278 us -> 278 us (level)
  no operation moved by 1% of the time
where the time goes in v10:
time: 278 us
  Pallas kernels  278 us (100%)
    pallas_call x1, Pallas kernels, local_block(): pl.pallas_call(kernel, out_shape=(pltpu.VMEM((BLOCK, D), jnp.bfloat16), p...  274 us

profile of v10, /device:TPU:1, one launch (start us, length us, event | category | flops | bytes accessed | tf_op | source)
XLA Modules:
  0.0 278.2 jit_solution(6151210308734118528)
XLA Ops:
  0.6 274.2 %mlp_reduce.1 = (bf16[1024,2048]{1,0:T(8,128)(2,1)S(1)}, bf16[1024,2048]{1,0:T(8,128)(2,1)S(1)}, f32[2,4,256,2048]{3,2,1,0:T(8,128)}, bf16[4,256,2048]{2,1,0:T(8,128)(2,1)}) custom-call(bf16[8192,2048]{1,0:T(8,128)(2,1)} %x_hbm.1, bf16[2048,1024]{1,0:T(8,128)(2,1)} %wg_hbm.1, bf16[2048,1024]{1,0:T(8,128)(2,1)} %wu_hbm.1, bf16[1024,2048]{1,0:T(8,128)(2,1)} %wd_hbm.1, ...), custom_call_target="tpu_custom_call" | custom-call | tf_op jit(solution)/shard_map/mlp_reduce/pallas_call | solution.py:290
  274.8 3.4 %store.1 = (bf16[1024,2048]{1,0:T(8,128)(2,1)}, bf16[1024,2048]{1,0:T(8,128)(2,1)}) custom-call(bf16[1024,2048]{1,0:T(8,128)(2,1)S(1)} %get-tuple-element.4.h_ref, bf16[1024,2048]{1,0:T(8,128)(2,1)S(1)} %get-tuple-element.5.n_ref), custom_call_target="tpu_custom_call" | custom-call | tf_op jit(solution)/shard_map/store/pallas_call | solution.py:332

commit v11 on v10

--- a/solution.py
+++ b/solution.py
@@ -27,7 +27,7 @@
 
 
 def kernel(x_hbm, wg_hbm, wu_hbm, wd_hbm, res_hbm, gain_hbm, h_ref, n_ref, sum_in, sib_own, x_buf, wg, wu, wd, wd_relay, hid, tiles, hid_in, sib_in, sum_out, sum_last, sum_ld, res_ld, sib_ld, gain_ref,
-           x_sem, w_sem, wr_sem, relay_sem, sib_ssem, sib_rsem, sum_ssem, sum_rsem, ld_sem, res_sem, sibld_sem, ready):
+           x_sem, w_sem, wr_sem, relay_sem, sib_ssem, sib_rsem, sum_ssem, sum_rsem, ready):
     me = lax.axis_index("tp")
     c, cx, cy = me % 2, (me // 2) % 2, me // 4
     sib = cy * 4 + cx * 2 + (1 - c)
@@ -35,7 +35,7 @@
     yn = (1 - cy) * 4 + cx * 2
 
     barrier = pltpu.get_barrier_semaphore()
-    source = (1 - c) * (yn + 1) + c * xn
+    source = (1 - c) * (xn + 1) + c * yn
     for dev in (sib, source):
         pl.semaphore_signal(barrier, inc=1, device_id={"tp": dev}, device_id_type=pl.DeviceIdType.MESH)
 
@@ -46,7 +46,7 @@
     def row_of(i):
         diag, to_sib, to_chip, kept = kinds(i)
         q = i % 4
-        direction = (1 - c) + (q // 2) * (2 * c - 1)
+        direction = c + (q // 2) * (1 - 2 * c)
         ty = diag * (1 - cy) + to_chip * (cy + direction * (1 - 2 * cy)) + (to_sib + kept) * cy
         tx = diag * (1 - cx) + to_chip * (cx + (1 - direction) * (1 - 2 * cx)) + (to_sib + kept) * cx
         tc = (diag + to_chip) * (i % 2) + to_sib * (1 - c) + kept * c
@@ -61,7 +61,7 @@
         copy.start()
     x_copy(0).start()
 
-    out_chip = (1 - c) * xn + c * yn
+    out_chip = (1 - c) * yn + c * xn
 
     def w_relay_copy(n):
         rows = (pl.ds(0, 128), pl.ds(128, F - 128))[n]
@@ -135,13 +135,13 @@
             sib_copy(j, 0, 0).wait_send()
 
         def res_copy():
-            return pltpu.make_async_copy(res_hbm.at[pl.ds(pl.multiple_of(k_own * ROWS, ROWS), ROWS)], res_ld, res_sem)
+            return pltpu.make_async_copy(res_hbm.at[pl.ds(pl.multiple_of(k_own * ROWS, ROWS), ROWS)], res_ld, w_sem.at[2])
 
         def sib_load():
-            return pltpu.make_async_copy(sib_own.at[k_own], sib_ld, sibld_sem)
+            return pltpu.make_async_copy(sib_own.at[k_own], sib_ld, w_sem.at[3])
 
         def sum_load(d, rows):
-            return pltpu.make_async_copy(sum_in.at[d, k_own, pl.ds(0, rows)], sum_ld.at[d, pl.ds(0, rows)], ld_sem.at[d])
+            return pltpu.make_async_copy(sum_in.at[d, k_own, pl.ds(0, rows)], sum_ld.at[d, pl.ds(0, rows)], w_sem.at[d])
 
         late_own = jnp.logical_and(k_own == last, c == 1)
 
@@ -272,11 +272,7 @@
 
 
 def store_kernel(h_ref, n_ref, h_hbm, n_hbm, sem):
-    copies = []
-    for b in range(4):
-        rows = pl.ds(b * (BLOCK // 4), BLOCK // 4)
-        copies.append(pltpu.make_async_copy(h_ref.at[rows], h_hbm.at[rows], sem.at[0, b]))
-        copies.append(pltpu.make_async_copy(n_ref.at[rows], n_hbm.at[rows], sem.at[1, b]))
+    copies = [pltpu.make_async_copy(h_ref, h_hbm, sem.at[0]), pltpu.make_async_copy(n_ref, n_hbm, sem.at[1])]
     for copy in copies:
         copy.start()
     for copy in copies:
@@ -321,9 +317,6 @@
                 pltpu.SemaphoreType.DMA((3, STEPS)),
                 pltpu.SemaphoreType.DMA((2, SUM_SLOTS + 2)),
                 pltpu.SemaphoreType.DMA((2, STEPS + 2)),
-                pltpu.SemaphoreType.DMA((2,)),
-                pltpu.SemaphoreType.DMA,
-                pltpu.SemaphoreType.DMA,
                 pltpu.SemaphoreType.REGULAR,
             ],
             compiler_params=pltpu.CompilerParams(collective_id=0, has_side_effects=True, vmem_limit_bytes=58000000),
@@ -334,7 +327,7 @@
             out_shape=(jax.ShapeDtypeStruct((BLOCK, D), jnp.bfloat16), jax.ShapeDtypeStruct((BLOCK, D), jnp.bfloat16)),
             in_specs=[vmem, vmem],
             out_specs=(hbm, hbm),
-            scratch_shapes=[pltpu.SemaphoreType.DMA((2, 4))],
+            scratch_shapes=[pltpu.SemaphoreType.DMA((2,))],
             compiler_params=pltpu.CompilerParams(vmem_limit_bytes=1048576),
             name="store",
         )(*(pltpu.with_memory_space_constraint(a, pltpu.VMEM) for a in (h, n)))

time: 278 us -> 278 us (level)
  no operation moved by 1% of the time
where the time goes in v11:
time: 278 us
  Pallas kernels  278 us (100%)
    pallas_call x1, Pallas kernels, local_block(): pl.pallas_call(kernel, out_shape=(pltpu.VMEM((BLOCK, D), jnp.bfloat16), p...  274 us

profile of v11, /device:TPU:1, one launch (start us, length us, event | category | flops | bytes accessed | tf_op | source)
XLA Modules:
  0.0 278.2 jit_solution(15661003975392131322)
XLA Ops:
  0.6 274.2 %mlp_reduce.1 = (bf16[1024,2048]{1,0:T(8,128)(2,1)S(1)}, bf16[1024,2048]{1,0:T(8,128)(2,1)S(1)}, f32[2,4,256,2048]{3,2,1,0:T(8,128)}, bf16[4,256,2048]{2,1,0:T(8,128)(2,1)}) custom-call(bf16[8192,2048]{1,0:T(8,128)(2,1)} %x_hbm.1, bf16[2048,1024]{1,0:T(8,128)(2,1)} %wg_hbm.1, bf16[2048,1024]{1,0:T(8,128)(2,1)} %wu_hbm.1, bf16[1024,2048]{1,0:T(8,128)(2,1)} %wd_hbm.1, ...), custom_call_target="tpu_custom_call" | custom-call | tf_op jit(solution)/shard_map/mlp_reduce/pallas_call | solution.py:286
  274.8 3.4 %store.1 = (bf16[1024,2048]{1,0:T(8,128)(2,1)}, bf16[1024,2048]{1,0:T(8,128)(2,1)}) custom-call(bf16[1024,2048]{1,0:T(8,128)(2,1)S(1)} %get-tuple-element.4.h_ref, bf16[1024,2048]{1,0:T(8,128)(2,1)S(1)} %get-tuple-element.5.n_ref), custom_call_target="tpu_custom_call" | custom-call | tf_op jit(solution)/shard_map/store/pallas_call | solution.py:325

commit v12 on v11

--- a/solution.py
+++ b/solution.py
@@ -272,11 +272,12 @@
 
 
 def store_kernel(h_ref, n_ref, h_hbm, n_hbm, sem):
-    copies = [pltpu.make_async_copy(h_ref, h_hbm, sem.at[0]), pltpu.make_async_copy(n_ref, n_hbm, sem.at[1])]
-    for copy in copies:
-        copy.start()
-    for copy in copies:
-        copy.wait()
+    for b in range(8):
+        rows = pl.ds(b * (BLOCK // 8), BLOCK // 8)
+        pltpu.make_async_copy(h_ref.at[rows], h_hbm.at[rows], sem.at[0]).start()
+        pltpu.make_async_copy(n_ref.at[rows], n_hbm.at[rows], sem.at[1]).start()
+    pltpu.make_async_copy(h_ref, h_hbm, sem.at[0]).wait()
+    pltpu.make_async_copy(n_ref, n_hbm, sem.at[1]).wait()
 
 
 def solution(mesh):

time: 278 us -> 278 us (level)
  no operation moved by 1% of the time
where the time goes in v12:
time: 278 us
  Pallas kernels  277 us (100%)
    pallas_call x1, Pallas kernels, local_block(): pl.pallas_call(kernel, out_shape=(pltpu.VMEM((BLOCK, D), jnp.bfloat16), p...  274 us

profile of v12, /device:TPU:1, one launch (start us, length us, event | category | flops | bytes accessed | tf_op | source)
XLA Modules:
  0.0 278.1 jit_solution(1185202124081765154)
XLA Ops:
  0.6 274.2 %mlp_reduce.1 = (bf16[1024,2048]{1,0:T(8,128)(2,1)S(1)}, bf16[1024,2048]{1,0:T(8,128)(2,1)S(1)}, f32[2,4,256,2048]{3,2,1,0:T(8,128)}, bf16[4,256,2048]{2,1,0:T(8,128)(2,1)}) custom-call(bf16[8192,2048]{1,0:T(8,128)(2,1)} %x_hbm.1, bf16[2048,1024]{1,0:T(8,128)(2,1)} %wg_hbm.1, bf16[2048,1024]{1,0:T(8,128)(2,1)} %wu_hbm.1, bf16[1024,2048]{1,0:T(8,128)(2,1)} %wd_hbm.1, ...), custom_call_target="tpu_custom_call" | custom-call | tf_op jit(solution)/shard_map/mlp_reduce/pallas_call | solution.py:287
  274.8 3.3 %store.1 = (bf16[1024,2048]{1,0:T(8,128)(2,1)}, bf16[1024,2048]{1,0:T(8,128)(2,1)}) custom-call(bf16[1024,2048]{1,0:T(8,128)(2,1)S(1)} %get-tuple-element.4.h_ref, bf16[1024,2048]{1,0:T(8,128)(2,1)S(1)} %get-tuple-element.5.n_ref), custom_call_target="tpu_custom_call" | custom-call | tf_op jit(solution)/shard_map/store/pallas_call | solution.py:326

commit v13 on v12

--- a/solution.py
+++ b/solution.py
@@ -272,8 +272,8 @@
 
 
 def store_kernel(h_ref, n_ref, h_hbm, n_hbm, sem):
-    for b in range(8):
-        rows = pl.ds(b * (BLOCK // 8), BLOCK // 8)
+    for b in range(16):
+        rows = pl.ds(b * (BLOCK // 16), BLOCK // 16)
         pltpu.make_async_copy(h_ref.at[rows], h_hbm.at[rows], sem.at[0]).start()
         pltpu.make_async_copy(n_ref.at[rows], n_hbm.at[rows], sem.at[1]).start()
     pltpu.make_async_copy(h_ref, h_hbm, sem.at[0]).wait()

time: 278 us -> 278 us (level)
  no operation moved by 1% of the time
where the time goes in v13:
time: 278 us
  Pallas kernels  277 us (100%)
    pallas_call x1, Pallas kernels, local_block(): pl.pallas_call(kernel, out_shape=(pltpu.VMEM((BLOCK, D), jnp.bfloat16), p...  274 us

profile of v13, /device:TPU:1, one launch (start us, length us, event | category | flops | bytes accessed | tf_op | source)
XLA Modules:
  0.0 278.1 jit_solution(13071320539876378366)
XLA Ops:
  0.6 274.2 %mlp_reduce.1 = (bf16[1024,2048]{1,0:T(8,128)(2,1)S(1)}, bf16[1024,2048]{1,0:T(8,128)(2,1)S(1)}, f32[2,4,256,2048]{3,2,1,0:T(8,128)}, bf16[4,256,2048]{2,1,0:T(8,128)(2,1)}) custom-call(bf16[8192,2048]{1,0:T(8,128)(2,1)} %x_hbm.1, bf16[2048,1024]{1,0:T(8,128)(2,1)} %wg_hbm.1, bf16[2048,1024]{1,0:T(8,128)(2,1)} %wu_hbm.1, bf16[1024,2048]{1,0:T(8,128)(2,1)} %wd_hbm.1, ...), custom_call_target="tpu_custom_call" | custom-call | tf_op jit(solution)/shard_map/mlp_reduce/pallas_call | solution.py:287
  274.8 3.3 %store.1 = (bf16[1024,2048]{1,0:T(8,128)(2,1)}, bf16[1024,2048]{1,0:T(8,128)(2,1)}) custom-call(bf16[1024,2048]{1,0:T(8,128)(2,1)S(1)} %get-tuple-element.4.h_ref, bf16[1024,2048]{1,0:T(8,128)(2,1)S(1)} %get-tuple-element.5.n_ref), custom_call_target="tpu_custom_call" | custom-call | tf_op jit(solution)/shard_map/store/pallas_call | solution.py:326

commit v14 on v13

--- a/solution.py
+++ b/solution.py
@@ -36,7 +36,7 @@
 
     barrier = pltpu.get_barrier_semaphore()
     source = (1 - c) * (xn + 1) + c * yn
-    for dev in (sib, source):
+    for dev in (source, sib):
         pl.semaphore_signal(barrier, inc=1, device_id={"tp": dev}, device_id_type=pl.DeviceIdType.MESH)
 
     def kinds(i):
@@ -94,12 +94,12 @@
         slot = k % SUM_SLOTS
         return pltpu.make_async_remote_copy(
             src_ref=sum_out.at[j, slot] if part is None else sum_out.at[j, slot, pl.ds(*parts[part])], dst_ref=landing(c, k, part),
-            send_sem=sum_ssem.at[j, slot + (part or 0)], recv_sem=sum_rsem.at[c, k + (part or 0)],
+            send_sem=sum_ssem.at[j * SUM_SLOTS + slot + (part or 0)], recv_sem=sum_rsem.at[c, k + (part or 0)],
             device_id={"tp": out_chip + j}, device_id_type=pl.DeviceIdType.MESH)
 
     def sum_arrival(d, k, part=None):
         return pltpu.make_async_remote_copy(
-            src_ref=landing(d, k, part), dst_ref=landing(d, k, part), send_sem=sum_ssem.at[0, 0], recv_sem=sum_rsem.at[d, k + (part or 0)],
+            src_ref=landing(d, k, part), dst_ref=landing(d, k, part), send_sem=sum_ssem.at[0], recv_sem=sum_rsem.at[d, k + (part or 0)],
             device_id={"tp": sib}, device_id_type=pl.DeviceIdType.MESH)
 
     pl.semaphore_wait(barrier, 2)
@@ -272,8 +272,8 @@
 
 
 def store_kernel(h_ref, n_ref, h_hbm, n_hbm, sem):
-    for b in range(16):
-        rows = pl.ds(b * (BLOCK // 16), BLOCK // 16)
+    for b in range(32):
+        rows = pl.ds(b * (BLOCK // 32), BLOCK // 32)
         pltpu.make_async_copy(h_ref.at[rows], h_hbm.at[rows], sem.at[0]).start()
         pltpu.make_async_copy(n_ref.at[rows], n_hbm.at[rows], sem.at[1]).start()
     pltpu.make_async_copy(h_ref, h_hbm, sem.at[0]).wait()
@@ -316,7 +316,7 @@
                 pltpu.SemaphoreType.DMA((2, FIRST // GROUP)),
                 pltpu.SemaphoreType.DMA((2,)),
                 pltpu.SemaphoreType.DMA((3, STEPS)),
-                pltpu.SemaphoreType.DMA((2, SUM_SLOTS + 2)),
+                pltpu.SemaphoreType.DMA((2 * SUM_SLOTS + 2,)),
                 pltpu.SemaphoreType.DMA((2, STEPS + 2)),
                 pltpu.SemaphoreType.REGULAR,
             ],

time: 278 us -> 278 us (level)
  no operation moved by 1% of the time
where the time goes in v14:
time: 278 us
  Pallas kernels  277 us (100%)
    pallas_call x1, Pallas kernels, local_block(): pl.pallas_call(kernel, out_shape=(pltpu.VMEM((BLOCK, D), jnp.bfloat16), p...  274 us

profile of v14, /device:TPU:1, one launch (start us, length us, event | category | flops | bytes accessed | tf_op | source)
XLA Modules:
  0.0 278.0 jit_solution(4449609970164333559)
XLA Ops:
  0.6 274.1 %mlp_reduce.1 = (bf16[1024,2048]{1,0:T(8,128)(2,1)S(1)}, bf16[1024,2048]{1,0:T(8,128)(2,1)S(1)}, f32[2,4,256,2048]{3,2,1,0:T(8,128)}, bf16[4,256,2048]{2,1,0:T(8,128)(2,1)}) custom-call(bf16[8192,2048]{1,0:T(8,128)(2,1)} %x_hbm.1, bf16[2048,1024]{1,0:T(8,128)(2,1)} %wg_hbm.1, bf16[2048,1024]{1,0:T(8,128)(2,1)} %wu_hbm.1, bf16[1024,2048]{1,0:T(8,128)(2,1)} %wd_hbm.1, ...), custom_call_target="tpu_custom_call" | custom-call | tf_op jit(solution)/shard_map/mlp_reduce/pallas_call | solution.py:287
  274.8 3.2 %store.1 = (bf16[1024,2048]{1,0:T(8,128)(2,1)}, bf16[1024,2048]{1,0:T(8,128)(2,1)}) custom-call(bf16[1024,2048]{1,0:T(8,128)(2,1)S(1)} %get-tuple-element.4.h_ref, bf16[1024,2048]{1,0:T(8,128)(2,1)S(1)} %get-tuple-element.5.n_ref), custom_call_target="tpu_custom_call" | custom-call | tf_op jit(solution)/shard_map/store/pallas_call | solution.py:326

commit v15 on v14

--- a/solution.py
+++ b/solution.py
@@ -272,8 +272,8 @@
 
 
 def store_kernel(h_ref, n_ref, h_hbm, n_hbm, sem):
-    for b in range(32):
-        rows = pl.ds(b * (BLOCK // 32), BLOCK // 32)
+    for b in range(64):
+        rows = pl.ds(b * (BLOCK // 64), BLOCK // 64)
         pltpu.make_async_copy(h_ref.at[rows], h_hbm.at[rows], sem.at[0]).start()
         pltpu.make_async_copy(n_ref.at[rows], n_hbm.at[rows], sem.at[1]).start()
     pltpu.make_async_copy(h_ref, h_hbm, sem.at[0]).wait()

time: 278 us -> 278 us (level)
  no operation moved by 1% of the time
where the time goes in v15:
time: 278 us
  Pallas kernels  277 us (100%)
    pallas_call x1, Pallas kernels, local_block(): pl.pallas_call(kernel, out_shape=(pltpu.VMEM((BLOCK, D), jnp.bfloat16), p...  274 us

profile of v15, /device:TPU:1, one launch (start us, length us, event | category | flops | bytes accessed | tf_op | source)
XLA Modules:
  0.0 278.0 jit_solution(8929027683726279858)
XLA Ops:
  0.6 274.1 %mlp_reduce.1 = (bf16[1024,2048]{1,0:T(8,128)(2,1)S(1)}, bf16[1024,2048]{1,0:T(8,128)(2,1)S(1)}, f32[2,4,256,2048]{3,2,1,0:T(8,128)}, bf16[4,256,2048]{2,1,0:T(8,128)(2,1)}) custom-call(bf16[8192,2048]{1,0:T(8,128)(2,1)} %x_hbm.1, bf16[2048,1024]{1,0:T(8,128)(2,1)} %wg_hbm.1, bf16[2048,1024]{1,0:T(8,128)(2,1)} %wu_hbm.1, bf16[1024,2048]{1,0:T(8,128)(2,1)} %wd_hbm.1, ...), custom_call_target="tpu_custom_call" | custom-call | tf_op jit(solution)/shard_map/mlp_reduce/pallas_call | solution.py:287
  274.8 3.2 %store.1 = (bf16[1024,2048]{1,0:T(8,128)(2,1)}, bf16[1024,2048]{1,0:T(8,128)(2,1)}) custom-call(bf16[1024,2048]{1,0:T(8,128)(2,1)S(1)} %get-tuple-element.4.h_ref, bf16[1024,2048]{1,0:T(8,128)(2,1)S(1)} %get-tuple-element.5.n_ref), custom_call_target="tpu_custom_call" | custom-call | tf_op jit(solution)/shard_map/store/pallas_call | solution.py:326
